TPU v7x, 512 devices: a 4x2x32 block of a 4x8x32 slice. The times are simulated.
512 devices in a mesh: parts: 2 (over y), expert: 64 (over z, core), tensor: 4 (over x).
Axes of the slice: x: 4, y: 2, z: 32, core: 2. Of those that a mesh axis runs over, the one named last changes fastest.
The devices are a block of a 4x8x32 slice.
Arguments:
- tokens: bfloat16 [2048, 6144], P(('parts', 'expert'), 'tensor'), parts along dimension 0, may hold values from -4 to 4
- queries: bfloat16 [2048, 48, 128], P(('parts', 'expert'), 'tensor'), parts along dimension 0, may hold values from -6 to 6
- new_kv: bfloat16 [2, 2048, 8, 128], P(None, ('parts', 'expert'), 'tensor'), parts along dimension 1, may hold values from -6 to 6
- cache_kv: bfloat16 [2, 2048, 16, 8, 128], P(None, ('parts', 'expert'), None, 'tensor'), parts along dimension 1, may hold values from -6 to 6
- lengths: int32 [2048], P(('parts', 'expert')), parts along dimension 0, may hold values from 2 to 16
- gain: float32 [6144], P('tensor'), may hold values from 0.1 to 1.9
- gate_weight: bfloat16 [6144, 32768], P('tensor', 'expert'), may hold values from -0.078125 to 0.078125
- up_weight: bfloat16 [6144, 32768], P('tensor', 'expert'), may hold values from -0.078125 to 0.078125
- down_weight: bfloat16 [32768, 6144], P('expert', 'tensor'), may hold values from -0.0625 to 0.0625
- routes: int32 [2048, 2], P(('parts', 'expert')), parts along dimension 0, may hold values from 0 to 3, all different within a row; in each aligned block of 16 rows (0 to 15, 16 to 31, ...) at most 9 rows name the same one
- route_weights: bfloat16 [2048, 2], P(('parts', 'expert')), parts along dimension 0, may hold values from 0.19921875 to 0.796875
Outputs:
- mixed: bfloat16 [2048, 6144], P(('parts', 'expert'), 'tensor'), parts along dimension 0
There are 2 independent parts, one for each index of `parts`. A program takes and returns all parts, laid end to end along the dimension named above; an argument that names none is the same for every part. Nothing has to cross between parts.
Inputs may be any that keep to these rules, and one draw needn't show every extreme that they name: `routes`: the two entries of a row differ; in the rows of one index of expert no expert is named more than 9 times, a bound that some block reaches there in every draw.
All inputs are finite; a program needn't handle non-finite values.
Results may differ from a plain program's by a relative error of at most 0.0094.
Values may be sent and summed in bfloat16 or wider, within the bound.
No kernel may reach another device: no remote copies, remote signals or barrier semaphores. Data moves between devices by JAX's collectives and lax.ppermute only.
A program may use at most 64 MiB of HBM per device.

v0:
```python
import math

import jax
import jax.numpy as jnp
from jax import lax
from jax.sharding import Mesh
from jax.sharding import PartitionSpec as P

EXPERTS = 4
CAP = 9
EXPERT = ("expert_0", "expert_1")
PARTS_EXPERT = ("parts", "expert_0", "expert_1")


EPSILON = 1e-05


def in_blocks(x, dim, count):
    lengths = x.shape
    blocks = x.reshape(*lengths[:dim], count, lengths[dim] // count, *lengths[dim + 1 :])
    return jnp.moveaxis(blocks, dim, 0)


def sent_and_summed(x, axis, dim):
    blocks = in_blocks(x, dim, lax.axis_size(axis))
    arrived = lax.all_to_all(blocks, axis, split_axis=0, concat_axis=0, tiled=True)
    return arrived.astype(jnp.float32).sum(axis=0)


def sent_together(arrays, axis, dim, along):
    ends, at = ([], 0)
    for a in arrays[:-1]:
        at += a.shape[along]
        ends.append(at)
    both = jnp.concatenate(arrays, axis=along)
    return tuple(jnp.split(sent_and_summed(both, axis, dim), ends, axis=along))


def sent_to_all(x, axis):
    copies = jnp.broadcast_to(x, (lax.axis_size(axis), *x.shape))
    return lax.all_to_all(copies, axis, split_axis=0, concat_axis=0, tiled=True)


def joined_along(blocks, dim):
    lengths = list(blocks.shape[1:])
    lengths[dim] *= blocks.shape[0]
    return jnp.moveaxis(blocks, 0, dim).reshape(lengths)


def collect(x, axis, dim):
    blocks = sent_to_all(x, axis)
    return joined_along(blocks, dim)


def from_partner(x, axis, apart):
    return lax.ppermute(x, axis, [(i, i ^ 1 << apart) for i in range(lax.axis_size(axis))])


def exchange_in_order(blocks, axes, turns):
    lengths = [lax.axis_size(a) for a in axes]
    blocks = blocks.reshape(*lengths, *blocks.shape[1:])
    for k in turns:
        blocks = lax.all_to_all(blocks, axes[k], split_axis=k, concat_axis=k, tiled=True)
    return blocks.reshape(-1, *blocks.shape[len(axes) :])


def exchange_by_chip(x, groups, turns, split_dim, concat_dim):
    count = lax.axis_size(groups[0]) * lax.axis_size(groups[1])
    blocks = in_blocks(x, split_dim, count)
    return joined_along(exchange_in_order(blocks, groups, turns), concat_dim)


def attend(queries, new_kv, cache_kv, lengths):
    sequences, head_count, head_size = queries.shape
    key_heads = new_kv.shape[2]
    groups = head_count // key_heads
    factor = 1.0 / math.sqrt(head_size)
    query_grp = queries.reshape(sequences, key_heads, groups, head_size)
    score_old = (
        jnp.einsum("skgd,spkd->skgp", query_grp, cache_kv[0], preferred_element_type=jnp.float32)
        * factor
    )
    score_new = (
        jnp.einsum("skgd,skd->skg", query_grp, new_kv[0], preferred_element_type=jnp.float32)
        * factor
    )
    position = jnp.arange(cache_kv.shape[2], dtype=jnp.int32)
    usable = (position[None, :] < lengths[:, None])[:, None, None, :]
    score_old = jnp.where(usable, score_old, -jnp.inf)
    largest = jnp.maximum(jnp.max(score_old, axis=3), score_new)
    weight_old = jnp.exp(score_old - largest[..., None])
    weight_new = jnp.exp(score_new - largest)
    denominator = jnp.sum(weight_old, axis=3) + weight_new
    prob_old = (weight_old / denominator[..., None]).astype(jnp.bfloat16)
    prob_new = (weight_new / denominator).astype(jnp.bfloat16)
    attended = jnp.einsum(
        "skgp,spkd->skgd", prob_old, cache_kv[1], preferred_element_type=jnp.float32
    )
    attended = (
        attended
        + prob_new.astype(jnp.float32)[..., None] * new_kv[1].astype(jnp.float32)[:, :, None, :]
    )
    return attended.reshape(sequences, head_count * head_size)


def expert_hidden(token_rows, gate_weight, up_weight, down_weight):
    gate_sum = jnp.dot(token_rows, gate_weight, preferred_element_type=jnp.float32)
    lift_sum = jnp.dot(token_rows, up_weight, preferred_element_type=jnp.float32)
    gate_sum, lift_sum = sent_together(
        (gate_sum.astype(jnp.bfloat16), lift_sum.astype(jnp.bfloat16)), "tensor", 1, 0
    )
    hidden = (jax.nn.silu(gate_sum) * lift_sum).astype(jnp.bfloat16)
    hidden = collect(hidden, "tensor", 1)
    return jnp.dot(hidden, down_weight, preferred_element_type=jnp.float32)


def pack_slots(target, normed):
    slot_ids = jnp.arange(EXPERTS * CAP, dtype=jnp.int32)
    placing = (slot_ids[:, None, None] == target[None, :, :]).astype(jnp.float32)
    placing = jnp.sum(placing, axis=2).astype(jnp.bfloat16)
    packed = jnp.dot(placing, normed, preferred_element_type=jnp.float32).astype(jnp.bfloat16)
    return packed.reshape(EXPERTS, CAP, normed.shape[1])


def mix_slots(target, route_weights, per_slot):
    slot_ids = jnp.arange(EXPERTS * CAP, dtype=jnp.int32)
    mixing = jnp.where(
        slot_ids[None, None, :] == target[:, :, None],
        route_weights.astype(jnp.float32)[:, :, None],
        jnp.float32(0.0),
    )
    mixing = jnp.sum(mixing, axis=1)
    return jnp.dot(
        mixing, per_slot, precision=lax.Precision.HIGHEST, preferred_element_type=jnp.float32
    )


def group_gather(blocks, position, bit_count):
    joined = blocks
    for bit in range(bit_count):
        partner = from_partner(joined, EXPERT, bit)
        upper = position >> bit & 1 == 1
        joined = jnp.where(
            upper,
            jnp.concatenate([partner, joined], axis=2),
            jnp.concatenate([joined, partner], axis=2),
        )
    return joined


def group_reduce(terms, position, bit_count):
    remaining = terms
    for bit in reversed(range(bit_count)):
        half = remaining.shape[2] // 2
        upper = position >> bit & 1
        keeping = lax.dynamic_slice_in_dim(remaining, upper * half, half, 2)
        sending = lax.dynamic_slice_in_dim(remaining, (1 - upper) * half, half, 2)
        remaining = keeping + from_partner(sending.astype(jnp.bfloat16), EXPERT, bit).astype(
            sending.dtype
        )
    return remaining


def on_device(
    tokens,
    queries,
    new_kv,
    cache_kv,
    lengths,
    gain,
    gate_weight,
    up_weight,
    down_weight,
    routes,
    route_weights,
):
    local_seqs, local_width = tokens.shape
    residual = tokens.astype(jnp.float32) + attend(queries, new_kv, cache_kv, lengths)
    full_width = local_width * lax.axis_size("tensor")
    squares = lax.psum(jnp.sum(residual * residual, axis=1), "tensor")
    normed = (residual * lax.rsqrt(squares[:, None] / full_width + EPSILON) * gain).astype(
        jnp.bfloat16
    )
    choosers = (routes[:, :, None] == jnp.arange(EXPERTS, dtype=jnp.int32)[None, None, :]).astype(
        jnp.int32
    )
    flat_choice = choosers.reshape(2 * local_seqs, EXPERTS)
    earlier = jnp.cumsum(flat_choice, axis=0) - flat_choice
    slot_index = jnp.sum(earlier * flat_choice, axis=1)
    target = (routes.reshape(-1) * CAP + slot_index).reshape(local_seqs, 2)
    devices = lax.axis_size(EXPERT)
    per_expert = devices // EXPERTS
    bit_count = per_expert.bit_length() - 1
    piece_width = local_width // per_expert
    position = lax.axis_index(EXPERT)
    packed = pack_slots(target, normed)
    outgoing = packed.reshape(EXPERTS, CAP, per_expert, piece_width).transpose(0, 2, 1, 3)
    outgoing = outgoing.reshape(devices, CAP, piece_width)
    arrived = exchange_by_chip(outgoing, ("expert_0", "expert_1"), (1, 0), 0, 0)
    sources = arrived.shape[0]
    items = arrived.shape[1]
    whole = group_gather(arrived.reshape(sources, items, 1, piece_width), position, bit_count)
    produced = expert_hidden(
        whole.reshape(sources * items, local_width), gate_weight, up_weight, down_weight
    )
    produced = produced.reshape(sources, items, per_expert, piece_width)
    summed = group_reduce(produced, position, bit_count)
    computed = summed.reshape(sources, items, piece_width)
    returned = lax.all_to_all(computed, EXPERT, split_axis=0, concat_axis=0, tiled=True)
    per_slot = returned.reshape(EXPERTS, per_expert, CAP, piece_width).transpose(0, 2, 1, 3)
    moe_sum = mix_slots(target, route_weights, per_slot.reshape(EXPERTS * CAP, local_width))
    return (residual + moe_sum).astype(jnp.bfloat16)


def solution(mesh):
    split = Mesh(
        mesh.devices.reshape(mesh.shape["parts"], 32, 2, mesh.shape["tensor"]),
        ("parts", "expert_0", "expert_1", "tensor"),
    )
    return jax.shard_map(
        on_device,
        mesh=split,
        in_specs=(
            P(PARTS_EXPERT, "tensor"),
            P(PARTS_EXPERT, "tensor", None),
            P(None, PARTS_EXPERT, "tensor", None),
            P(None, PARTS_EXPERT, None, "tensor", None),
            P(PARTS_EXPERT),
            P("tensor"),
            P("tensor", EXPERT),
            P("tensor", EXPERT),
            P(EXPERT, "tensor"),
            P(PARTS_EXPERT, None),
            P(PARTS_EXPERT, None),
        ),
        out_specs=P(PARTS_EXPERT, "tensor"),
        check_vma=False,
    )
```

profile of v0, /device:TPU:40, one launch (start us, length us, event | category | flops | bytes accessed | tf_op | source)
XLA Modules:
  0.0 484.7 jit_solution(6325391461054517430)
XLA Ops:
  0.0 1.3 fusion.18
  1.3 0.7 iota_compare_fusion.3
  2.0 0.7 slice_bitcast_fusion
  2.7 1.0 fusion.6
  3.7 1.1 fusion.19
  4.8 0.2 fusion.5
  5.1 0.3 convolution_add_fusion.1
  5.4 0.5 copy-done.3
  5.9 0.1 multiply_reduce_fusion
  6.0 10.9 %psum.7 = f32[16]{0:T(128)S(1)} all-reduce(f32[16]{0:T(128)S(1)} %multiply_reduce_fusion), channel_id=1, replica_groups=mesh['parts'=2,'expert_0'=32,'expert_1'=2,'tensor'=4] {'tensor'}, use_global_device_ids=true, to_apply=%region_7.8 | all-reduce | flops 16 | bytes 128 | tf_op jit(solution)/shard_map/psum | solution.py:180
  17.2 0.2 select_reduce_fusion.1
  17.7 0.2 convolution_convert_fusion
  17.9 0.1 reshape_reshape.3
  18.1 3.8 all_to_all.25
  22.1 78.1 %all_to_all.26 = bf16[32,2,1,9,96]{4,1,3,2,0:T(2,128)(2,1)S(1)} all-to-all(bf16[32,2,1,9,96]{4,1,3,2,0:T(2,128)(2,1)S(1)} %copy.87), channel_id=1, replica_groups=mesh['parts'=2,'expert_0'=32,'expert_1'=2,'tensor'=4] {'expert_0'}, dimensions={0} | all-to-all | bytes 221184 | tf_op jit(solution)/shard_map/all_to_all | solution.py:63
  100.3 2.0 collective-permute-start
  102.3 1.3 collective-permute-done
  103.7 2.2 collective-permute-start.1
  106.0 8.8 %collective-permute-done.1 = bf16[64,9,2,96]{3,0,1,2:T(8,128)(2,1)S(1)} collective-permute-done((bf16[64,9,2,96]{3,0,1,2:T(8,128)(2,1)S(1)}, bf16[64,9,2,96]{3,0,1,2:T(8,128)(2,1)S(1)}, u32[]{:S(2)}, u32[]{:S(2)}) %collective-permute-start.1) | collective-permute-done | bytes 221216 | tf_op jit(solution)/shard_map/ppermute | solution.py:56
  114.7 0.3 maximum_select_fusion.2
  115.0 2.0 collective-permute-start.2
  116.9 27.9 %collective-permute-done.2 = bf16[64,9,4,96]{3,0,1,2:T(8,128)(2,1)} collective-permute-done((bf16[64,9,4,96]{3,0,1,2:T(8,128)(2,1)S(1)}, bf16[64,9,4,96]{3,0,1,2:T(8,128)(2,1)}, u32[]{:S(2)}, u32[]{:S(2)}) %collective-permute-start.2) | collective-permute-done | bytes 442400 | tf_op jit(solution)/shard_map/ppermute | solution.py:56
  144.8 1.7 maximum_select_fusion.1
  146.6 2.0 collective-permute-start.3
  148.5 103.6 %collective-permute-done.3 = bf16[64,9,8,96]{3,0,1,2:T(8,128)(2,1)} collective-permute-done((bf16[64,9,8,96]{3,0,1,2:T(8,128)(2,1)S(1)}, bf16[64,9,8,96]{3,0,1,2:T(8,128)(2,1)}, u32[]{:S(2)}, u32[]{:S(2)}) %collective-permute-start.3) | collective-permute-done | bytes 884768 | tf_op jit(solution)/shard_map/ppermute | solution.py:56
  252.2 2.3 maximum_select_fusion
  254.5 2.9 copy.89
  257.4 4.0 select_n.78
  261.5 1.1 convolution_convert_fusion.1
  262.6 0.3 copy-done.6
  262.9 1.1 convolution_convert_fusion.2
  264.0 0.2 bitcast_bitcast_fusion
  264.2 19.4 %all_to_all.27 = bf16[4,1152,128]{2,1,0:T(8,128)(2,1)S(1)} all-to-all(bf16[4,1152,128]{2,1,0:T(8,128)(2,1)S(1)} %bitcast_bitcast_fusion), channel_id=1, replica_groups=mesh['parts'=2,'expert_0'=32,'expert_1'=2,'tensor'=4] {'tensor'}, dimensions={0} | all-to-all | bytes 2359296 | tf_op jit(solution)/shard_map/all_to_all | solution.py:26
  283.6 0.2 convert_reduce_fusion
  283.9 0.9 broadcast_in_dim.26
  284.8 4.4 all-to-all-start.3
  289.2 1.7 copy.92
  290.9 7.9 %all-to-all-done.3 = bf16[4,576,128]{2,1,0:T(8,128)(2,1)} async-done(((bf16[4,576,128]{2,1,0:T(8,128)(2,1)}), bf16[4,576,128]{2,1,0:T(8,128)(2,1)}, u32[]{:S(2)}, u32[]{:S(2)}) %all-to-all-start.3) | async-done | bytes 589856 | tf_op jit(solution)/shard_map/all_to_all | solution.py:41
  298.8 2.3 copy.91
  301.1 2.3 dot_general.36
  303.4 2.7 fusion.2
  306.2 2.1 copy-done.1
  308.3 0.2 dynamic-slice_convert_fusion
  308.5 2.0 collective-permute-start.4
  310.5 75.3 %collective-permute-done.4 = bf16[64,9,8,96]{3,0,2,1:T(8,128)(2,1)} collective-permute-done((bf16[64,9,8,96]{3,0,2,1:T(8,128)(2,1)S(1)}, bf16[64,9,8,96]{3,0,2,1:T(8,128)(2,1)}, u32[]{:S(2)}, u32[]{:S(2)}) %collective-permute-start.4) | collective-permute-done | bytes 884768 | tf_op jit(solution)/shard_map/ppermute | solution.py:56
  385.8 2.4 convert_add_fusion
  388.2 1.4 copy-done.2
  389.7 2.0 collective-permute-start.5
  391.7 22.3 %collective-permute-done.5 = bf16[64,9,4,96]{3,0,2,1:T(8,128)(2,1)S(1)} collective-permute-done((bf16[64,9,4,96]{3,0,2,1:T(8,128)(2,1)S(1)}, bf16[64,9,4,96]{3,0,2,1:T(8,128)(2,1)S(1)}, u32[]{:S(2)}, u32[]{:S(2)}) %collective-permute-start.5) | collective-permute-done | bytes 442400 | tf_op jit(solution)/shard_map/ppermute | solution.py:56
  413.9 1.4 convert_add_fusion.1
  415.4 2.0 collective-permute-start.6
  417.4 9.0 %collective-permute-done.6 = bf16[64,9,2,96]{3,0,2,1:T(8,128)(2,1)} collective-permute-done((bf16[64,9,2,96]{3,0,2,1:T(8,128)(2,1)S(1)}, bf16[64,9,2,96]{3,0,2,1:T(8,128)(2,1)}, u32[]{:S(2)}, u32[]{:S(2)}) %collective-permute-start.6) | collective-permute-done | bytes 221216 | tf_op jit(solution)/shard_map/ppermute | solution.py:56
  426.4 1.0 convert_add_fusion.2
  427.5 2.0 collective-permute-start.7
  429.4 1.3 collective-permute-done.7
  430.8 0.2 copy.94
  431.0 1.1 reshape.89
  432.1 10.6 %all-to-all-start.4 = ((f32[64,1,864]{2,1,0:T(1,128)}), f32[64,1,864]{2,1,0:T(1,128)S(1)}, u32[]{:S(2)}, u32[]{:S(2)}) async-start(f32[64,1,864]{2,1,0:T(1,128)} %reshape.89), calls=%async_computation.4 | async-start | bytes 458752 | tf_op jit(solution)/shard_map/all_to_all | solution.py:209
  442.8 38.9 %all-to-all-done.4 = f32[64,1,864]{2,1,0:T(1,128)S(1)} async-done(((f32[64,1,864]{2,1,0:T(1,128)}), f32[64,1,864]{2,1,0:T(1,128)S(1)}, u32[]{:S(2)}, u32[]{:S(2)}) %all-to-all-start.4) | async-done | bytes 221216 | tf_op jit(solution)/shard_map/all_to_all | solution.py:209
  481.7 0.5 broadcast.46
  482.2 1.2 reduce
  483.4 0.2 reshape.90
  483.7 0.2 reshape.83
  483.8 0.9 fusion
  (37 shorter events, 1.5 us)
Async XLA Ops:
  0.0 261.5 %copy-start = (bf16[1536,512]{1,0:T(8,128)(2,1)S(1)}, bf16[1536,512]{1,0:T(8,128)(2,1)}, u32[]{:S(2)}) copy-start(bf16[1536,512]{1,0:T(8,128)(2,1)} %param.18) | copy-start | bytes 4718596
  5.1 0.8 copy-start.3
  5.1 11.9 %copy-start.5 = (s32[16,2]{0,1:T(2,128)S(1)}, s32[16,2]{0,1:T(2,128)}, u32[]{:S(2)}) copy-start(s32[16,2]{0,1:T(2,128)} %param.20) | copy-start | bytes 388
  5.1 12.6 %copy-start.4 = (f32[1536]{0:T(1024)S(1)}, f32[1536]{0:T(1024)}, u32[]{:S(2)}) copy-start(f32[1536]{0:T(1024)} %param.16) | copy-start | bytes 18436
  100.3 3.3 collective-permute-start
  103.7 11.0 %collective-permute-start.1 = (bf16[64,9,2,96]{3,0,1,2:T(8,128)(2,1)S(1)}, bf16[64,9,2,96]{3,0,1,2:T(8,128)(2,1)S(1)}, u32[]{:S(2)}, u32[]{:S(2)}) collective-permute-start(bf16[64,9,2,96]{3,0,1,2:T(8,128)(2,1)S(1)} %maximum_select_fusion.3), channel_id=1, source_target_pairs={{0,8},{4,12},{8,0},{12,4},{16,24},{20,28},{24,16},{28,20},{32,40},... | collective-permute-start | bytes 663560 | tf_op jit(solution)/shard_map/ppermute | solution.py:56
  115.0 29.8 %collective-permute-start.2 = (bf16[64,9,4,96]{3,0,1,2:T(8,128)(2,1)S(1)}, bf16[64,9,4,96]{3,0,1,2:T(8,128)(2,1)}, u32[]{:S(2)}, u32[]{:S(2)}) collective-permute-start(bf16[64,9,4,96]{3,0,1,2:T(8,128)(2,1)S(1)} %maximum_select_fusion.2), channel_id=1, source_target_pairs={{0,16},{4,20},{8,24},{12,28},{16,0},{20,4},{24,8},{28,12},{32,48},... | collective-permute-start | bytes 1327112 | tf_op jit(solution)/shard_map/ppermute | solution.py:56
  146.6 105.6 %collective-permute-start.3 = (bf16[64,9,8,96]{3,0,1,2:T(8,128)(2,1)S(1)}, bf16[64,9,8,96]{3,0,1,2:T(8,128)(2,1)}, u32[]{:S(2)}, u32[]{:S(2)}) collective-permute-start(bf16[64,9,8,96]{3,0,1,2:T(8,128)(2,1)S(1)} %maximum_select_fusion.1), channel_id=1, source_target_pairs={{0,32},{4,36},{8,40},{12,44},{16,48},{20,52},{24,56},{28,60},{32,0... | collective-permute-start | bytes 2654216 | tf_op jit(solution)/shard_map/ppermute | solution.py:56
  261.5 1.4 copy-start.6
  284.8 14.0 %all-to-all-start.3 = ((bf16[4,576,128]{2,1,0:T(8,128)(2,1)}), bf16[4,576,128]{2,1,0:T(8,128)(2,1)}, u32[]{:S(2)}, u32[]{:S(2)}) async-start(bf16[4,576,128]{2,1,0:T(8,128)(2,1)} %broadcast_in_dim.26), calls=%async_computation.3 | async-start | bytes 1179648 | tf_op jit(solution)/shard_map/all_to_all | solution.py:41
  306.2 2.1 copy-start.1
  308.5 77.3 %collective-permute-start.4 = (bf16[64,9,8,96]{3,0,2,1:T(8,128)(2,1)S(1)}, bf16[64,9,8,96]{3,0,2,1:T(8,128)(2,1)}, u32[]{:S(2)}, u32[]{:S(2)}) collective-permute-start(bf16[64,9,8,96]{3,0,2,1:T(8,128)(2,1)S(1)} %dynamic-slice_convert_fusion), channel_id=1, source_target_pairs={{0,32},{4,36},{8,40},{12,44},{16,48},{20,52},{24,56},{28,60},{32,0... | collective-permute-start | bytes 2654216 | tf_op jit(solution)/shard_map/ppermute | solution.py:56
  388.2 1.4 copy-start.2
  389.7 24.2 %collective-permute-start.5 = (bf16[64,9,4,96]{3,0,2,1:T(8,128)(2,1)S(1)}, bf16[64,9,4,96]{3,0,2,1:T(8,128)(2,1)S(1)}, u32[]{:S(2)}, u32[]{:S(2)}) collective-permute-start(bf16[64,9,4,96]{3,0,2,1:T(8,128)(2,1)S(1)} %dynamic-slice_convert_fusion.1), channel_id=1, source_target_pairs={{0,16},{4,20},{8,24},{12,28},{16,0},{20,4},{24,8},{28,12},{32,48},... | collective-permute-start | bytes 1327112 | tf_op jit(solution)/shard_map/ppermute | solution.py:56
  415.4 11.0 %collective-permute-start.6 = (bf16[64,9,2,96]{3,0,2,1:T(8,128)(2,1)S(1)}, bf16[64,9,2,96]{3,0,2,1:T(8,128)(2,1)}, u32[]{:S(2)}, u32[]{:S(2)}) collective-permute-start(bf16[64,9,2,96]{3,0,2,1:T(8,128)(2,1)S(1)} %dynamic-slice_convert_fusion.2), channel_id=1, source_target_pairs={{0,8},{4,12},{8,0},{12,4},{16,24},{20,28},{24,16},{28,20},{32,40},... | collective-permute-start | bytes 663560 | tf_op jit(solution)/shard_map/ppermute | solution.py:56
  427.4 15.3 %copy-start.7 = (bf16[16,2]{0,1:T(2,128)(2,1)S(1)}, bf16[16,2]{0,1:T(2,128)(2,1)}, u32[]{:S(2)}) copy-start(bf16[16,2]{0,1:T(2,128)(2,1)} %param.21) | copy-start | bytes 196
  427.5 3.3 collective-permute-start.7
  432.1 49.6 %all-to-all-start.4 = ((f32[64,1,864]{2,1,0:T(1,128)}), f32[64,1,864]{2,1,0:T(1,128)S(1)}, u32[]{:S(2)}, u32[]{:S(2)}) async-start(f32[64,1,864]{2,1,0:T(1,128)} %reshape.89), calls=%async_computation.4 | async-start | bytes 458752 | tf_op jit(solution)/shard_map/all_to_all | solution.py:209
where the time goes:
time: 486 us; the launch traced here: 485 us
  waiting for transfers between devices  296 us (61%)
  blocking collectives  112 us (23%)
  starting transfers between devices  30.9 us (6%)
  local copies, waits for them, and re-layouts  23.2 us (5%)
  other arithmetic  13.2 us (3%)
  matrix products  8.28 us (2%)
    ppermute x8, waiting for transfers between devices, from_partner(): lax.ppermute(x, axis, [(i, i ^ 1 << apart) for i in range(lax.axis_size(a...  250 us
    all_to_all x2, blocking collectives, exchange_in_order(): lax.all_to_all(blocks, axes[k], split_axis=k, concat_axis=k, tiled=True)  82 us
    all_to_all x1, waiting for transfers between devices, on_device(): lax.all_to_all(computed, EXPERT, split_axis=0, concat_axis=0, tiled=True)  38.9 us
    all_to_all x1, blocking collectives, sent_and_summed(): lax.all_to_all(blocks, axis, split_axis=0, concat_axis=0, tiled=True)  19.4 us
    ppermute x8, starting transfers between devices, from_partner(): lax.ppermute(x, axis, [(i, i ^ 1 << apart) for i in range(lax.axis_size(a...  15.9 us
    psum x1, blocking collectives, on_device(): squares = lax.psum(jnp.sum(residual * residual, axis=1), 'tensor')  10.9 us
    all_to_all x1, starting transfers between devices, on_device(): lax.all_to_all(computed, EXPERT, split_axis=0, concat_axis=0, tiled=True)  10.6 us
  transfers between devices with their start and end apart: 10, of which 10 were waited for; matrix products, arithmetic and copies ran while one was open for 0% of the time, Pallas kernels for 0%

commit v1 on v0

v1 whole, which is shorter than its diff:
```python
import math

import jax
import jax.numpy as jnp
from jax import lax
from jax.sharding import Mesh
from jax.sharding import PartitionSpec as P

EXPERTS = 4
CAP = 9
EXPERT = ("seg", "pos", "core")
PARTS_EXPERT = ("parts", "seg", "pos", "core")
LANES = 128

EPSILON = 1e-05


def shifted(x, axis, by):
    count = lax.axis_size(axis)
    return lax.ppermute(x, axis, [(i, (i + by) % count) for i in range(count)])


def from_partner(x, axis, apart):
    return lax.ppermute(x, axis, [(i, i ^ apart) for i in range(lax.axis_size(axis))])


def attend(queries, new_kv, cache_kv, lengths):
    sequences, head_count, head_size = queries.shape
    key_heads = new_kv.shape[2]
    groups = head_count // key_heads
    factor = 1.0 / math.sqrt(head_size)
    query_grp = queries.reshape(sequences, key_heads, groups, head_size)
    score_old = (
        jnp.einsum("skgd,spkd->skgp", query_grp, cache_kv[0], preferred_element_type=jnp.float32)
        * factor
    )
    score_new = (
        jnp.einsum("skgd,skd->skg", query_grp, new_kv[0], preferred_element_type=jnp.float32)
        * factor
    )
    position = jnp.arange(cache_kv.shape[2], dtype=jnp.int32)
    usable = (position[None, :] < lengths[:, None])[:, None, None, :]
    score_old = jnp.where(usable, score_old, -jnp.inf)
    largest = jnp.maximum(jnp.max(score_old, axis=3), score_new)
    weight_old = jnp.exp(score_old - largest[..., None])
    weight_new = jnp.exp(score_new - largest)
    denominator = jnp.sum(weight_old, axis=3) + weight_new
    prob_old = (weight_old / denominator[..., None]).astype(jnp.bfloat16)
    prob_new = (weight_new / denominator).astype(jnp.bfloat16)
    attended = jnp.einsum(
        "skgp,spkd->skgd", prob_old, cache_kv[1], preferred_element_type=jnp.float32
    )
    attended = (
        attended
        + prob_new.astype(jnp.float32)[..., None] * new_kv[1].astype(jnp.float32)[:, :, None, :]
    )
    return attended.reshape(sequences, head_count * head_size)


def doubled(rows, axis, apart):
    return jnp.concatenate([rows, from_partner(rows, axis, apart)], axis=0)


def halved(terms, axis, apart):
    half = terms.shape[0] // 2
    arrived = from_partner(terms[half:].astype(jnp.bfloat16), axis, apart)
    return terms[:half] + arrived.astype(jnp.float32)


def exchanged(blocks, back):
    sign = -1 if back else 1
    return jnp.stack(
        [blocks[0]] + [shifted(blocks[r], "seg", sign * r) for r in range(1, EXPERTS)]
    )


def expert_part(rows, gain, gate_weight, up_weight, down_weight):
    count, local_width = rows.shape
    columns = gate_weight.shape[1]
    across = lax.axis_size("tensor")
    plain = rows.astype(jnp.float32) / gain
    squares = jnp.sum(plain * plain, axis=1, keepdims=True)
    squares_high = lax.reduce_precision(squares, 8, 7)
    squares_low = squares - squares_high
    lane = lax.broadcasted_iota(jnp.int32, (count, LANES), 1)
    squares = jnp.where(lane == 0, squares_high, squares_low).astype(jnp.bfloat16)
    gate_sum = jnp.dot(rows, gate_weight, preferred_element_type=jnp.float32)
    lift_sum = jnp.dot(rows, up_weight, preferred_element_type=jnp.float32)
    sums = jnp.concatenate(
        [gate_sum.astype(jnp.bfloat16), lift_sum.astype(jnp.bfloat16), squares], axis=1
    )
    sums = sums.reshape(across, count // across, sums.shape[1])
    sums = lax.all_to_all(sums, "tensor", split_axis=0, concat_axis=0, tiled=True)
    sums = jnp.sum(sums.astype(jnp.float32), axis=0)
    squares = sums[:, 2 * columns : 2 * columns + 1] + sums[:, 2 * columns + 1 : 2 * columns + 2]
    scale = lax.rsqrt(squares / (local_width * across) + EPSILON)
    hidden = jax.nn.silu(sums[:, :columns] * scale) * (sums[:, columns : 2 * columns] * scale)
    hidden = hidden.astype(jnp.bfloat16)
    copies = jnp.broadcast_to(hidden, (across, *hidden.shape))
    hidden = lax.all_to_all(copies, "tensor", split_axis=0, concat_axis=0, tiled=True)
    hidden = hidden.reshape(count, columns)
    return jnp.dot(hidden, down_weight, preferred_element_type=jnp.float32)


def on_device(
    tokens,
    queries,
    new_kv,
    cache_kv,
    lengths,
    gain,
    gate_weight,
    up_weight,
    down_weight,
    routes,
    route_weights,
):
    local_seqs, local_width = tokens.shape
    residual = tokens.astype(jnp.float32) + attend(queries, new_kv, cache_kv, lengths)
    scaled = (residual * gain).astype(jnp.bfloat16)
    ahead = (routes - lax.axis_index("seg") + EXPERTS) % EXPERTS
    choosers = (ahead[:, :, None] == jnp.arange(EXPERTS, dtype=jnp.int32)[None, None, :]).astype(
        jnp.int32
    )
    flat_choice = choosers.reshape(2 * local_seqs, EXPERTS)
    earlier = jnp.cumsum(flat_choice, axis=0) - flat_choice
    slot_index = jnp.sum(earlier * flat_choice, axis=1)
    target = (ahead.reshape(-1) * CAP + slot_index).reshape(local_seqs, 2)
    slot_ids = jnp.arange(EXPERTS * CAP, dtype=jnp.int32)
    placing = jnp.sum(
        (slot_ids[:, None, None] == target[None, :, :]).astype(jnp.float32), axis=2
    ).astype(jnp.bfloat16)
    mixing = jnp.sum(
        jnp.where(
            slot_ids[None, None, :] == target[:, :, None],
            route_weights.astype(jnp.float32)[:, :, None],
            jnp.float32(0.0),
        ),
        axis=1,
    ).astype(jnp.bfloat16)
    packed = jnp.dot(placing, scaled, preferred_element_type=jnp.float32).astype(jnp.bfloat16)
    flat = (EXPERTS, CAP * local_width // LANES, LANES)
    rows = exchanged(packed.reshape(flat), False).reshape(EXPERTS * CAP, local_width)
    distances = [1 << bit for bit in range(lax.axis_size("pos").bit_length() - 1)]
    for apart in reversed(distances):
        rows = doubled(rows, "pos", apart)
    rows = doubled(rows, "core", 1)
    produced = expert_part(rows, gain, gate_weight, up_weight, down_weight)
    produced = halved(produced, "core", 1)
    for apart in distances:
        produced = halved(produced, "pos", apart)
    returned = exchanged(produced.astype(jnp.bfloat16).reshape(flat), True)
    per_slot = returned.reshape(EXPERTS * CAP, local_width)
    moe_sum = jnp.dot(mixing, per_slot, preferred_element_type=jnp.float32)
    return (residual + moe_sum).astype(jnp.bfloat16)


def solution(mesh):
    split = Mesh(
        mesh.devices.reshape(
            mesh.shape["parts"], EXPERTS, mesh.shape["expert"] // (2 * EXPERTS), 2, mesh.shape["tensor"]
        ),
        ("parts", "seg", "pos", "core", "tensor"),
    )
    return jax.shard_map(
        on_device,
        mesh=split,
        in_specs=(
            P(PARTS_EXPERT, "tensor"),
            P(PARTS_EXPERT, "tensor", None),
            P(None, PARTS_EXPERT, "tensor", None),
            P(None, PARTS_EXPERT, None, "tensor", None),
            P(PARTS_EXPERT),
            P("tensor"),
            P("tensor", EXPERT),
            P("tensor", EXPERT),
            P(EXPERT, "tensor"),
            P(PARTS_EXPERT, None),
            P(PARTS_EXPERT, None),
        ),
        out_specs=P(PARTS_EXPERT, "tensor"),
        check_vma=False,
    )
```

time: 486 us -> 266 us (0.55)
  waiting for transfers between devices: 296 us -> 86.1 us
  starting transfers between devices: 30.9 us -> 121 us
  blocking collectives: 112 us -> 34.8 us
  local copies, waits for them, and re-layouts: 23.2 us -> 11.7 us
  other arithmetic: 13.2 us -> 4.23 us
    ppermute x8 -> x14, waiting for transfers between devices: 250 us -> 86.1 us  [the longest x8 64.5 us: from_partner(): lax.ppermute(x, axis, [(i, i ^ apart) for i in range(lax.axis_size(axis))])]
    ppermute x8 -> x14, starting transfers between devices: 15.9 us -> 121 us  [the longest x6 88.3 us: shifted(): return lax.ppermute(x, axis, [(i, (i + by) % count) for i in range(count)])]
    all_to_all x3 -> x2, blocking collectives: 101 us -> 34.8 us  [the longest x1 22.8 us: expert_part(): lax.all_to_all(sums, 'tensor', split_axis=0, concat_axis=0, tiled=True)]
    all_to_all x2 -> x0, waiting for transfers between devices: 46.7 us -> none  [the longest x1 38.9 us: on_device(): lax.all_to_all(computed, EXPERT, split_axis=0, concat_axis=0, tiled=True)]
    all_to_all x2 -> x0, starting transfers between devices: 15.1 us -> none  [the longest x1 10.6 us: on_device(): lax.all_to_all(computed, EXPERT, split_axis=0, concat_axis=0, tiled=True)]
    psum x1 -> x0, blocking collectives: 10.9 us -> none  [on_device(): squares = lax.psum(jnp.sum(residual * residual, axis=1), 'tensor')]
    concatenate x0 -> x1, local copies, waits for them, and re-layouts: none -> 7.68 us  [doubled(): return jnp.concatenate([rows, from_partner(rows, axis, apart)], axis=0)]
    select_n x2 -> x1, local copies, waits for them, and re-layouts: 6.96 us -> 0.09 us  [on_device(): ahead = (routes - lax.axis_index('seg') + EXPERTS) % EXPERTS]
  transfers between devices with their start and end apart: 10 -> 14, of which waited for: 10 -> 11; matrix products, arithmetic and copies ran while one was open for 0% -> 0% of each run, Pallas kernels for 0% -> 0%
where the time goes in v1:
time: 266 us; the launch traced here: 265 us
  starting transfers between devices  121 us (45%)
  waiting for transfers between devices  86.1 us (32%)
  blocking collectives  34.8 us (13%)
  local copies, waits for them, and re-layouts  11.7 us (4%)
  matrix products  6.5 us (2%)
  other arithmetic  4.23 us (2%)
    ppermute x6, starting transfers between devices, shifted(): return lax.ppermute(x, axis, [(i, (i + by) % count) for i in range(count)])  88.3 us
    ppermute x8, waiting for transfers between devices, from_partner(): lax.ppermute(x, axis, [(i, i ^ apart) for i in range(lax.axis_size(axis))])  64.5 us
    ppermute x8, starting transfers between devices, from_partner(): lax.ppermute(x, axis, [(i, i ^ apart) for i in range(lax.axis_size(axis))])  32.6 us
    all_to_all x1, blocking collectives, expert_part(): lax.all_to_all(sums, 'tensor', split_axis=0, concat_axis=0, tiled=True)  22.8 us
    ppermute x6, waiting for transfers between devices, shifted(): return lax.ppermute(x, axis, [(i, (i + by) % count) for i in range(count)])  21.6 us
    all_to_all x1, blocking collectives, expert_part(): lax.all_to_all(copies, 'tensor', split_axis=0, concat_axis=0, tiled=True)  12 us
    concatenate x1, local copies, waits for them, and re-layouts, doubled(): return jnp.concatenate([rows, from_partner(rows, axis, apart)], axis=0)  7.68 us
  transfers between devices with their start and end apart: 14, of which 11 were waited for; matrix products, arithmetic and copies ran while one was open for 0% of the time, Pallas kernels for 0%

profile of v1, /device:TPU:40, one launch (start us, length us, event | category | flops | bytes accessed | tf_op | source)
XLA Modules:
  0.0 264.7 jit_solution(17481292748725577041)
XLA Ops:
  0.0 1.3 fusion.23
  1.3 0.7 iota_compare_fusion.3
  2.0 0.7 slice_bitcast_fusion
  2.7 1.0 fusion.10
  3.7 1.1 fusion.27
  4.8 0.2 fusion.5
  5.1 0.3 convolution_add_fusion.1
  5.5 0.1 copy.41
  5.6 0.1 eq.52
  5.7 0.1 fusion.16
  5.8 0.2 select_reduce_fusion.1
  6.0 0.1 reduce_sum.58
  6.0 0.1 copy.42
  6.2 0.1 convert_reduce_fusion.1
  6.3 0.2 convolution_convert_fusion
  6.5 0.1 squeeze.33
  6.6 43.6 %collective-permute-start.2 = (bf16[108,128]{1,0:T(8,128)(2,1)S(1)}, bf16[108,128]{1,0:T(8,128)(2,1)S(1)}, u32[]{:S(2)}, u32[]{:S(2)}) collective-permute-start(bf16[108,128]{1,0:T(8,128)(2,1)S(1)} %squeeze.33), channel_id=1, source_target_pairs={{0,192},{64,0},{128,64},{192,128},{1,193},{65,1},{129,65},{193,129... | collective-permute-start | bytes 82952 | tf_op jit(solution)/shard_map/ppermute | solution.py:20
  50.3 2.0 collective-permute-start
  52.3 12.1 %collective-permute-start.1 = (bf16[108,128]{1,0:T(8,128)(2,1)S(1)}, bf16[108,128]{1,0:T(8,128)(2,1)S(1)}, u32[]{:S(2)}, u32[]{:S(2)}) collective-permute-start(bf16[108,128]{1,0:T(8,128)(2,1)S(1)} %squeeze.32), channel_id=1, source_target_pairs={{0,128},{64,192},{128,0},{192,64},{1,129},{65,193},{129,1},{193,65... | collective-permute-start | bytes 82952 | tf_op jit(solution)/shard_map/ppermute | solution.py:20
  64.5 4.1 %collective-permute-done = bf16[108,128]{1,0:T(8,128)(2,1)S(1)} collective-permute-done((bf16[108,128]{1,0:T(8,128)(2,1)S(1)}, bf16[108,128]{1,0:T(8,128)(2,1)S(1)}, u32[]{:S(2)}, u32[]{:S(2)}) %collective-permute-start) | collective-permute-done | bytes 27680 | tf_op jit(solution)/shard_map/ppermute | solution.py:20
  68.7 7.9 %collective-permute-done.1 = bf16[108,128]{1,0:T(8,128)(2,1)S(1)} collective-permute-done((bf16[108,128]{1,0:T(8,128)(2,1)S(1)}, bf16[108,128]{1,0:T(8,128)(2,1)S(1)}, u32[]{:S(2)}, u32[]{:S(2)}) %collective-permute-start.1) | collective-permute-done | bytes 27680 | tf_op jit(solution)/shard_map/ppermute | solution.py:20
  76.6 0.2 reshape.90
  76.7 7.7 %collective-permute-start.3 = (bf16[36,1536]{1,0:T(8,128)(2,1)S(1)}, bf16[36,1536]{1,0:T(8,128)(2,1)S(1)}, u32[]{:S(2)}, u32[]{:S(2)}) collective-permute-start(bf16[36,1536]{1,0:T(8,128)(2,1)S(1)} %reshape.90), channel_id=1, source_target_pairs={{0,32},{8,40},{16,48},{24,56},{32,0},{40,8},{48,16},{56,24},{1,33}... | collective-permute-start | bytes 331784 | tf_op jit(solution)/shard_map/ppermute | solution.py:24
  84.4 10.6 %collective-permute-done.3 = bf16[36,1536]{1,0:T(8,128)(2,1)S(1)} collective-permute-done((bf16[36,1536]{1,0:T(8,128)(2,1)S(1)}, bf16[36,1536]{1,0:T(8,128)(2,1)S(1)}, u32[]{:S(2)}, u32[]{:S(2)}) %collective-permute-start.3) | collective-permute-done | bytes 110624 | tf_op jit(solution)/shard_map/ppermute | solution.py:24
  95.0 2.0 collective-permute-start.4
  97.0 9.8 %collective-permute-done.4 = bf16[72,1536]{1,0:T(8,128)(2,1)S(1)} collective-permute-done((bf16[72,1536]{1,0:T(8,128)(2,1)S(1)}, bf16[72,1536]{1,0:T(8,128)(2,1)S(1)}, u32[]{:S(2)}, u32[]{:S(2)}) %collective-permute-start.4) | collective-permute-done | bytes 221216 | tf_op jit(solution)/shard_map/ppermute | solution.py:24
  106.8 2.0 collective-permute-start.5
  108.7 10.1 %collective-permute-done.5 = bf16[144,1536]{1,0:T(8,128)(2,1)S(1)} collective-permute-done((bf16[144,1536]{1,0:T(8,128)(2,1)S(1)}, bf16[144,1536]{1,0:T(8,128)(2,1)S(1)}, u32[]{:S(2)}, u32[]{:S(2)}) %collective-permute-start.5) | collective-permute-done | bytes 442400 | tf_op jit(solution)/shard_map/ppermute | solution.py:24
  118.8 0.1 pad_maximum_fusion.1
  118.9 2.0 collective-permute-start.6
  120.9 2.5 collective-permute-done.6
  123.4 7.7 %concatenate.21 = bf16[576,1536]{1,0:T(8,128)(2,1)S(1)} concatenate(bf16[36,1536]{1,0:T(8,128)(2,1)S(1)} %reshape.90, bf16[36,1536]{1,0:T(8,128)(2,1)} %copy-done.2, bf16[72,1536]{1,0:T(8,128)(2,1)} %copy-done.1, bf16[144,1536]{1,0:T(8,128)(2,1)} %copy-done.3, bf16[288,1536]{1,0:T(8,128)(2,1)} %collective-permute-done.6), dimensions={0} | concatenate | bytes 3538944 | tf_op jit(solution)/shard_map/concatenate | solution.py:61
  131.1 0.5 multiply_reduce_fusion
  131.6 0.8 copy-done.9
  132.5 1.1 convolution_convert_fusion.1
  133.5 0.3 copy-done.10
  133.9 1.1 convolution_convert_fusion.2
  135.0 0.2 select_convert_fusion
  135.2 0.1 pad_maximum_fusion
  135.3 22.8 %all_to_all.10 = bf16[4,144,1152]{2,1,0:T(8,128)(2,1)S(1)} all-to-all(bf16[4,144,1152]{2,1,0:T(8,128)(2,1)S(1)} %bitcast.34), channel_id=1, replica_groups=mesh['parts'=2,'seg'=4,'pos'=8,'core'=2,'tensor'=4] {'tensor'}, dimensions={0} | all-to-all | bytes 2654208 | tf_op jit(solution)/shard_map/all_to_all | solution.py:93
  158.1 0.2 convert_reduce_fusion
  158.2 0.2 fusion.9
  158.4 0.2 fusion.3
  158.6 12.0 %all_to_all.11 = bf16[4,144,512]{2,1,0:T(8,128)(2,1)S(1)} all-to-all(bf16[4,144,512]{2,1,0:T(8,128)(2,1)S(1)} %broadcast_in_dim.64), channel_id=1, replica_groups=mesh['parts'=2,'seg'=4,'pos'=8,'core'=2,'tensor'=4] {'tensor'}, dimensions={0} | all-to-all | bytes 1179648 | tf_op jit(solution)/shard_map/all_to_all | solution.py:100
  170.7 1.1 fusion.28
  171.8 0.1 slice.164
  171.9 2.0 collective-permute-start.7
  173.8 2.4 collective-permute-done.7
  176.2 0.2 slice_add_fusion
  176.5 3.7 %collective-permute-start.8 = (bf16[144,1536]{1,0:T(8,128)(2,1)S(1)}, bf16[144,1536]{1,0:T(8,128)(2,1)S(1)}, u32[]{:S(2)}, u32[]{:S(2)}) collective-permute-start(bf16[144,1536]{1,0:T(8,128)(2,1)S(1)} %slice.165), channel_id=1, source_target_pairs={{0,8},{8,0},{16,24},{24,16},{32,40},{40,32},{48,56},{56,48},{1,9},... | collective-permute-start | bytes 1327112 | tf_op jit(solution)/shard_map/ppermute | solution.py:24
  180.2 10.5 %collective-permute-done.8 = bf16[144,1536]{1,0:T(8,128)(2,1)S(1)} collective-permute-done((bf16[144,1536]{1,0:T(8,128)(2,1)S(1)}, bf16[144,1536]{1,0:T(8,128)(2,1)S(1)}, u32[]{:S(2)}, u32[]{:S(2)}) %collective-permute-start.8) | collective-permute-done | bytes 442400 | tf_op jit(solution)/shard_map/ppermute | solution.py:24
  190.7 0.1 slice_add_fusion.1
  190.8 5.3 %collective-permute-start.9 = (bf16[72,1536]{1,0:T(8,128)(2,1)S(1)}, bf16[72,1536]{1,0:T(8,128)(2,1)S(1)}, u32[]{:S(2)}, u32[]{:S(2)}) collective-permute-start(bf16[72,1536]{1,0:T(8,128)(2,1)S(1)} %slice.166), channel_id=1, source_target_pairs={{0,16},{8,24},{16,0},{24,8},{32,48},{40,56},{48,32},{56,40},{1,17}... | collective-permute-start | bytes 663560 | tf_op jit(solution)/shard_map/ppermute | solution.py:24
  196.1 9.6 %collective-permute-done.9 = bf16[72,1536]{1,0:T(8,128)(2,1)S(1)} collective-permute-done((bf16[72,1536]{1,0:T(8,128)(2,1)S(1)}, bf16[72,1536]{1,0:T(8,128)(2,1)S(1)}, u32[]{:S(2)}, u32[]{:S(2)}) %collective-permute-start.9) | collective-permute-done | bytes 221216 | tf_op jit(solution)/shard_map/ppermute | solution.py:24
  205.8 8.2 %collective-permute-start.10 = (bf16[36,1536]{1,0:T(8,128)(2,1)S(1)}, bf16[36,1536]{1,0:T(8,128)(2,1)S(1)}, u32[]{:S(2)}, u32[]{:S(2)}) collective-permute-start(bf16[36,1536]{1,0:T(8,128)(2,1)S(1)} %slice.167), channel_id=1, source_target_pairs={{0,32},{8,40},{16,48},{24,56},{32,0},{40,8},{48,16},{56,24},{1,33}... | collective-permute-start | bytes 331784 | tf_op jit(solution)/shard_map/ppermute | solution.py:24
  214.0 9.2 %collective-permute-done.10 = bf16[36,1536]{1,0:T(8,128)(2,1)S(1)} collective-permute-done((bf16[36,1536]{1,0:T(8,128)(2,1)S(1)}, bf16[36,1536]{1,0:T(8,128)(2,1)S(1)}, u32[]{:S(2)}, u32[]{:S(2)}) %collective-permute-start.10) | collective-permute-done | bytes 110624 | tf_op jit(solution)/shard_map/ppermute | solution.py:24
  223.4 15.9 %collective-permute-start.11 = (bf16[108,128]{1,0:T(8,128)(2,1)S(1)}, bf16[108,128]{1,0:T(8,128)(2,1)S(1)}, u32[]{:S(2)}, u32[]{:S(2)}) collective-permute-start(bf16[108,128]{1,0:T(8,128)(2,1)S(1)} %squeeze.34), channel_id=1, source_target_pairs={{0,192},{64,0},{128,64},{192,128},{1,193},{65,1},{129,65},{193,129... | collective-permute-start | bytes 82952 | tf_op jit(solution)/shard_map/ppermute | solution.py:20
  239.3 0.1 squeeze.35
  239.3 2.0 collective-permute-start.12
  241.4 12.7 %collective-permute-start.13 = (bf16[108,128]{1,0:T(8,128)(2,1)S(1)}, bf16[108,128]{1,0:T(8,128)(2,1)S(1)}, u32[]{:S(2)}, u32[]{:S(2)}) collective-permute-start(bf16[108,128]{1,0:T(8,128)(2,1)S(1)} %squeeze.36), channel_id=1, source_target_pairs={{0,64},{64,128},{128,192},{192,0},{1,65},{65,129},{129,193},{193,1... | collective-permute-start | bytes 82952 | tf_op jit(solution)/shard_map/ppermute | solution.py:20
  254.1 0.1 select_reduce_fusion
  254.2 9.5 %collective-permute-done.12 = bf16[108,128]{1,0:T(8,128)(2,1)S(1)} collective-permute-done((bf16[108,128]{1,0:T(8,128)(2,1)S(1)}, bf16[108,128]{1,0:T(8,128)(2,1)S(1)}, u32[]{:S(2)}, u32[]{:S(2)}) %collective-permute-start.12) | collective-permute-done | bytes 27680 | tf_op jit(solution)/shard_map/ppermute | solution.py:20
  263.8 0.2 reshape.93
  264.0 0.8 fusion
  (52 shorter events, 1.1 us)
Async XLA Ops:
  0.0 170.7 %copy-start = (bf16[512,1536]{1,0:T(8,128)(2,1)S(1)}, bf16[512,1536]{1,0:T(8,128)(2,1)}, u32[]{:S(2)}) copy-start(bf16[512,1536]{1,0:T(8,128)(2,1)} %param.19) | copy-start | bytes 4718596
  4.8 0.7 copy-start.8
  4.8 1.4 copy-start.6
  4.8 1.4 copy-start.7
  5.4 71.2 %copy-start.4 = (f32[16,1536]{1,0:T(8,128)}, f32[16,1536]{1,0:T(8,128)S(1)}, u32[]{:S(2)}) copy-start(f32[16,1536]{1,0:T(8,128)S(1)} %reshape.89) | copy-start | bytes 294916
  6.6 58.0 %collective-permute-start.2 = (bf16[108,128]{1,0:T(8,128)(2,1)S(1)}, bf16[108,128]{1,0:T(8,128)(2,1)S(1)}, u32[]{:S(2)}, u32[]{:S(2)}) collective-permute-start(bf16[108,128]{1,0:T(8,128)(2,1)S(1)} %squeeze.33), channel_id=1, source_target_pairs={{0,192},{64,0},{128,64},{192,128},{1,193},{65,1},{129,65},{193,129... | collective-permute-start | bytes 82952 | tf_op jit(solution)/shard_map/ppermute | solution.py:20
  50.3 18.4 %collective-permute-start = (bf16[108,128]{1,0:T(8,128)(2,1)S(1)}, bf16[108,128]{1,0:T(8,128)(2,1)S(1)}, u32[]{:S(2)}, u32[]{:S(2)}) collective-permute-start(bf16[108,128]{1,0:T(8,128)(2,1)S(1)} %squeeze.31), channel_id=1, source_target_pairs={{0,64},{64,128},{128,192},{192,0},{1,65},{65,129},{129,193},{193,1... | collective-permute-start | bytes 82952 | tf_op jit(solution)/shard_map/ppermute | solution.py:20
  52.3 24.2 %collective-permute-start.1 = (bf16[108,128]{1,0:T(8,128)(2,1)S(1)}, bf16[108,128]{1,0:T(8,128)(2,1)S(1)}, u32[]{:S(2)}, u32[]{:S(2)}) collective-permute-start(bf16[108,128]{1,0:T(8,128)(2,1)S(1)} %squeeze.32), channel_id=1, source_target_pairs={{0,128},{64,192},{128,0},{192,64},{1,129},{65,193},{129,1},{193,65... | collective-permute-start | bytes 82952 | tf_op jit(solution)/shard_map/ppermute | solution.py:20
  76.7 18.2 %collective-permute-start.3 = (bf16[36,1536]{1,0:T(8,128)(2,1)S(1)}, bf16[36,1536]{1,0:T(8,128)(2,1)S(1)}, u32[]{:S(2)}, u32[]{:S(2)}) collective-permute-start(bf16[36,1536]{1,0:T(8,128)(2,1)S(1)} %reshape.90), channel_id=1, source_target_pairs={{0,32},{8,40},{16,48},{24,56},{32,0},{40,8},{48,16},{56,24},{1,33}... | collective-permute-start | bytes 331784 | tf_op jit(solution)/shard_map/ppermute | solution.py:24
  95.0 25.9 %copy-start.2 = (bf16[36,1536]{1,0:T(8,128)(2,1)}, bf16[36,1536]{1,0:T(8,128)(2,1)S(1)}, u32[]{:S(2)}) copy-start(bf16[36,1536]{1,0:T(8,128)(2,1)S(1)} %collective-permute-done.3) | copy-start | bytes 331780
  95.0 11.7 %collective-permute-start.4 = (bf16[72,1536]{1,0:T(8,128)(2,1)S(1)}, bf16[72,1536]{1,0:T(8,128)(2,1)S(1)}, u32[]{:S(2)}, u32[]{:S(2)}) collective-permute-start(bf16[72,1536]{1,0:T(8,128)(2,1)S(1)} %pad_maximum_fusion.3), channel_id=1, source_target_pairs={{0,16},{8,24},{16,0},{24,8},{32,48},{40,56},{48,32},{56,40},{1,17}... | collective-permute-start | bytes 663560 | tf_op jit(solution)/shard_map/ppermute | solution.py:24
  106.7 14.1 %copy-start.1 = (bf16[72,1536]{1,0:T(8,128)(2,1)}, bf16[72,1536]{1,0:T(8,128)(2,1)S(1)}, u32[]{:S(2)}) copy-start(bf16[72,1536]{1,0:T(8,128)(2,1)S(1)} %collective-permute-done.4) | copy-start | bytes 663556
  106.8 12.0 %collective-permute-start.5 = (bf16[144,1536]{1,0:T(8,128)(2,1)S(1)}, bf16[144,1536]{1,0:T(8,128)(2,1)S(1)}, u32[]{:S(2)}, u32[]{:S(2)}) collective-permute-start(bf16[144,1536]{1,0:T(8,128)(2,1)S(1)} %pad_maximum_fusion.2), channel_id=1, source_target_pairs={{0,8},{8,0},{16,24},{24,16},{32,40},{40,32},{48,56},{56,48},{1,9},... | collective-permute-start | bytes 1327112 | tf_op jit(solution)/shard_map/ppermute | solution.py:24
  118.8 2.1 copy-start.3
  118.9 4.5 %collective-permute-start.6 = (bf16[288,1536]{1,0:T(8,128)(2,1)S(1)}, bf16[288,1536]{1,0:T(8,128)(2,1)}, u32[]{:S(2)}, u32[]{:S(2)}) collective-permute-start(bf16[288,1536]{1,0:T(8,128)(2,1)S(1)} %pad_maximum_fusion.1), channel_id=1, source_target_pairs={{0,4},{4,0},{1,5},{5,1},{2,6},{6,2},{3,7},{7,3},{8,12},{12,8},{9,1... | collective-permute-start | bytes 2654216 | tf_op jit(solution)/shard_map/ppermute | solution.py:24
  131.1 1.4 copy-start.9
  132.5 1.4 copy-start.10
  171.9 4.4 %collective-permute-start.7 = (bf16[288,1536]{1,0:T(8,128)(2,1)S(1)}, bf16[288,1536]{1,0:T(8,128)(2,1)S(1)}, u32[]{:S(2)}, u32[]{:S(2)}) collective-permute-start(bf16[288,1536]{1,0:T(8,128)(2,1)S(1)} %slice.164), channel_id=1, source_target_pairs={{0,4},{4,0},{1,5},{5,1},{2,6},{6,2},{3,7},{7,3},{8,12},{12,8},{9,1... | collective-permute-start | bytes 2654216 | tf_op jit(solution)/shard_map/ppermute | solution.py:24
  176.5 37.5 %copy-start.11 = (bf16[16,2]{0,1:T(2,128)(2,1)S(1)}, bf16[16,2]{0,1:T(2,128)(2,1)}, u32[]{:S(2)}) copy-start(bf16[16,2]{0,1:T(2,128)(2,1)} %param.21) | copy-start | bytes 196
  176.5 14.1 %collective-permute-start.8 = (bf16[144,1536]{1,0:T(8,128)(2,1)S(1)}, bf16[144,1536]{1,0:T(8,128)(2,1)S(1)}, u32[]{:S(2)}, u32[]{:S(2)}) collective-permute-start(bf16[144,1536]{1,0:T(8,128)(2,1)S(1)} %slice.165), channel_id=1, source_target_pairs={{0,8},{8,0},{16,24},{24,16},{32,40},{40,32},{48,56},{56,48},{1,9},... | collective-permute-start | bytes 1327112 | tf_op jit(solution)/shard_map/ppermute | solution.py:24
  190.8 73.2 %copy-start.5 = (f32[16,1536]{1,0:T(8,128)S(1)}, f32[16,1536]{1,0:T(8,128)}, u32[]{:S(2)}) copy-start(f32[16,1536]{1,0:T(8,128)} %copy-done.4) | copy-start | bytes 294916
  190.8 14.9 %collective-permute-start.9 = (bf16[72,1536]{1,0:T(8,128)(2,1)S(1)}, bf16[72,1536]{1,0:T(8,128)(2,1)S(1)}, u32[]{:S(2)}, u32[]{:S(2)}) collective-permute-start(bf16[72,1536]{1,0:T(8,128)(2,1)S(1)} %slice.166), channel_id=1, source_target_pairs={{0,16},{8,24},{16,0},{24,8},{32,48},{40,56},{48,32},{56,40},{1,17}... | collective-permute-start | bytes 663560 | tf_op jit(solution)/shard_map/ppermute | solution.py:24
  205.8 17.4 %collective-permute-start.10 = (bf16[36,1536]{1,0:T(8,128)(2,1)S(1)}, bf16[36,1536]{1,0:T(8,128)(2,1)S(1)}, u32[]{:S(2)}, u32[]{:S(2)}) collective-permute-start(bf16[36,1536]{1,0:T(8,128)(2,1)S(1)} %slice.167), channel_id=1, source_target_pairs={{0,32},{8,40},{16,48},{24,56},{32,0},{40,8},{48,16},{56,24},{1,33}... | collective-permute-start | bytes 331784 | tf_op jit(solution)/shard_map/ppermute | solution.py:24
  223.4 30.9 %collective-permute-start.11 = (bf16[108,128]{1,0:T(8,128)(2,1)S(1)}, bf16[108,128]{1,0:T(8,128)(2,1)S(1)}, u32[]{:S(2)}, u32[]{:S(2)}) collective-permute-start(bf16[108,128]{1,0:T(8,128)(2,1)S(1)} %squeeze.34), channel_id=1, source_target_pairs={{0,192},{64,0},{128,64},{192,128},{1,193},{65,1},{129,65},{193,129... | collective-permute-start | bytes 82952 | tf_op jit(solution)/shard_map/ppermute | solution.py:20
  239.3 24.4 %collective-permute-start.12 = (bf16[108,128]{1,0:T(8,128)(2,1)S(1)}, bf16[108,128]{1,0:T(8,128)(2,1)S(1)}, u32[]{:S(2)}, u32[]{:S(2)}) collective-permute-start(bf16[108,128]{1,0:T(8,128)(2,1)S(1)} %squeeze.35), channel_id=1, source_target_pairs={{0,128},{64,192},{128,0},{192,64},{1,129},{65,193},{129,1},{193,65... | collective-permute-start | bytes 82952 | tf_op jit(solution)/shard_map/ppermute | solution.py:20
  241.4 22.4 %collective-permute-start.13 = (bf16[108,128]{1,0:T(8,128)(2,1)S(1)}, bf16[108,128]{1,0:T(8,128)(2,1)S(1)}, u32[]{:S(2)}, u32[]{:S(2)}) collective-permute-start(bf16[108,128]{1,0:T(8,128)(2,1)S(1)} %squeeze.36), channel_id=1, source_target_pairs={{0,64},{64,128},{128,192},{192,0},{1,65},{65,129},{129,193},{193,1... | collective-permute-start | bytes 82952 | tf_op jit(solution)/shard_map/ppermute | solution.py:20

commit v2 on v1

v2 whole, which is shorter than its diff:
```python
import functools
import math

import jax
import jax.numpy as jnp
from jax import lax
from jax.experimental import pallas as pl
from jax.experimental.pallas import tpu as pltpu
from jax.sharding import Mesh
from jax.sharding import PartitionSpec as P


EXPERTS = 4
CAP = 9
EXPERT = ("seg", "pos", "core")
PARTS_EXPERT = ("parts", "seg", "pos", "core")
LANES = 128

EPSILON = 1e-05


def from_partner(x, axis, apart):
    return lax.ppermute(x, axis, [(i, i ^ apart) for i in range(lax.axis_size(axis))])


def attend(queries, new_kv, cache_kv, lengths):
    sequences, head_count, head_size = queries.shape
    key_heads = new_kv.shape[2]
    groups = head_count // key_heads
    factor = 1.0 / math.sqrt(head_size)
    query_grp = queries.reshape(sequences, key_heads, groups, head_size)
    score_old = (
        jnp.einsum("skgd,spkd->skgp", query_grp, cache_kv[0], preferred_element_type=jnp.float32)
        * factor
    )
    score_new = (
        jnp.einsum("skgd,skd->skg", query_grp, new_kv[0], preferred_element_type=jnp.float32)
        * factor
    )
    position = jnp.arange(cache_kv.shape[2], dtype=jnp.int32)
    usable = (position[None, :] < lengths[:, None])[:, None, None, :]
    score_old = jnp.where(usable, score_old, -jnp.inf)
    largest = jnp.maximum(jnp.max(score_old, axis=3), score_new)
    weight_old = jnp.exp(score_old - largest[..., None])
    weight_new = jnp.exp(score_new - largest)
    denominator = jnp.sum(weight_old, axis=3) + weight_new
    prob_old = (weight_old / denominator[..., None]).astype(jnp.bfloat16)
    prob_new = (weight_new / denominator).astype(jnp.bfloat16)
    attended = jnp.einsum(
        "skgp,spkd->skgd", prob_old, cache_kv[1], preferred_element_type=jnp.float32
    )
    attended = (
        attended
        + prob_new.astype(jnp.float32)[..., None] * new_kv[1].astype(jnp.float32)[:, :, None, :]
    )
    return attended.reshape(sequences, head_count * head_size)


def between_segments(blocks):
    segs, places, cores = (lax.axis_size(a) for a in EXPERT)
    groups = [
        [
            (seg * places + (place + places // 2 * (2 * seg // segs)) % places) * cores + core
            for seg in range(segs)
        ]
        for place in range(places)
        for core in range(cores)
    ]
    return lax.all_to_all(
        blocks, EXPERT, split_axis=0, concat_axis=0, tiled=True, axis_index_groups=groups
    )


def kept(x):
    return pltpu.with_memory_space_constraint(x, pltpu.VMEM)


def up_kernel(*refs):
    pieces, (gain_ref, gate_ref, up_ref, out_ref, rows_ref) = refs[:-5], refs[-5:]
    across, share, _ = out_ref.shape
    columns = gate_ref.shape[1]
    count = pieces[0].shape[0]
    inverse = 1.0 / gain_ref[...]
    lane = lax.broadcasted_iota(jnp.int32, (count, LANES), 1)
    for i, piece in enumerate(pieces):
        rows = piece[...]
        rows_ref[i * count : (i + 1) * count, :] = rows
        plain = rows.astype(jnp.float32) * inverse
        squares = jnp.sum(plain * plain, axis=1, keepdims=True)
        high = squares.astype(jnp.bfloat16).astype(jnp.float32)
        both = jnp.where(lane == 0, high, squares - high).astype(jnp.bfloat16)
        out_ref[i, :, 2 * columns :] = both
    for at, weight in ((0, gate_ref), (columns, up_ref)):
        sums = jnp.dot(rows_ref[...], weight[...], preferred_element_type=jnp.float32)
        sums = sums.astype(jnp.bfloat16)
        for i in range(across):
            out_ref[i, :, at : at + columns] = sums[i * share : (i + 1) * share]


def up_part(pieces, gain, gate_weight, up_weight):
    count, local_width = pieces[0].shape
    columns = gate_weight.shape[1]
    across = lax.axis_size("tensor")
    assert across == len(pieces)
    whole = pl.BlockSpec(memory_space=pltpu.VMEM)
    return pl.pallas_call(
        up_kernel,
        out_shape=pltpu.VMEM((across, count, 2 * columns + LANES), jnp.bfloat16),
        in_specs=[whole] * (len(pieces) + 3),
        out_specs=whole,
        scratch_shapes=[pltpu.VMEM((len(pieces) * count, local_width), jnp.bfloat16)],
        compiler_params=pltpu.CompilerParams(vmem_limit_bytes=16 << 20),
        name="up",
    )(*map(kept, (*pieces, gain.reshape(1, local_width), gate_weight, up_weight)))


def hidden_kernel(full_width, sums_ref, out_ref):
    across, _, width = sums_ref.shape
    columns = (width - LANES) // 2
    total = sums_ref[0].astype(jnp.float32)
    for i in range(1, across):
        total = total + sums_ref[i].astype(jnp.float32)
    squares = total[:, 2 * columns : 2 * columns + 1] + total[:, 2 * columns + 1 : 2 * columns + 2]
    scale = lax.rsqrt(squares / full_width + EPSILON)
    gate = total[:, :columns] * scale
    lift = total[:, columns : 2 * columns] * scale
    hidden = (gate / (1.0 + jnp.exp(-gate)) * lift).astype(jnp.bfloat16)
    for i in range(across):
        out_ref[i] = hidden


def activated(sums, full_width):
    across, count, width = sums.shape
    whole = pl.BlockSpec(memory_space=pltpu.VMEM)
    return pl.pallas_call(
        functools.partial(hidden_kernel, full_width),
        out_shape=pltpu.VMEM((across, count, (width - LANES) // 2), jnp.bfloat16),
        in_specs=[whole],
        out_specs=whole,
        compiler_params=pltpu.CompilerParams(vmem_limit_bytes=8 << 20),
        name="hidden",
    )(kept(sums))


def send(x):
    return x.astype(jnp.bfloat16)


def gathered(own):
    by4 = from_partner(own, "pos", 4)
    by2 = from_partner(own, "pos", 2)
    by6 = from_partner(by4, "pos", 2)
    near = jnp.concatenate([own, by4], axis=0)
    far = jnp.concatenate([by2, by6], axis=0)
    near_next = from_partner(near, "pos", 1)
    far_next = from_partner(far, "pos", 1)
    held = jnp.concatenate([near, far], axis=0)
    held_there = from_partner(held, "core", 1)
    following = jnp.concatenate([near_next, far_next], axis=0)
    following_there = from_partner(following, "core", 1)
    return held, following, held_there, following_there


def summed(terms):
    part = terms.shape[0] // 4
    held, following, held_there, following_there = (
        terms[i * part : (i + 1) * part] for i in range(4)
    )
    following = following + from_partner(send(following_there), "core", 1).astype(jnp.float32)
    held = held + from_partner(send(held_there), "core", 1).astype(jnp.float32)
    half = part // 2
    far = held[half:] + from_partner(send(following[half:]), "pos", 1).astype(jnp.float32)
    near = held[:half] + from_partner(send(following[:half]), "pos", 1).astype(jnp.float32)
    own = half // 2
    by4 = near[own:] + from_partner(send(far[own:]), "pos", 2).astype(jnp.float32)
    home = near[:own] + from_partner(send(far[:own]), "pos", 2).astype(jnp.float32)
    return home + from_partner(send(by4), "pos", 4).astype(jnp.float32)


def through_expert(pieces, gain, gate_weight, up_weight, down_weight):
    across = lax.axis_size("tensor")
    sums = up_part(pieces, gain, gate_weight, up_weight)
    sums = lax.all_to_all(sums, "tensor", split_axis=0, concat_axis=0, tiled=True)
    copies = activated(sums, gate_weight.shape[0] * across)
    hidden = lax.all_to_all(copies, "tensor", split_axis=0, concat_axis=0, tiled=True)
    hidden = hidden.reshape(-1, hidden.shape[2])
    return jnp.dot(hidden, down_weight, preferred_element_type=jnp.float32)


def on_device(
    tokens,
    queries,
    new_kv,
    cache_kv,
    lengths,
    gain,
    gate_weight,
    up_weight,
    down_weight,
    routes,
    route_weights,
):
    local_seqs, local_width = tokens.shape
    residual = tokens.astype(jnp.float32) + attend(queries, new_kv, cache_kv, lengths)
    scaled = (residual * gain).astype(jnp.bfloat16)
    choosers = (routes[:, :, None] == jnp.arange(EXPERTS, dtype=jnp.int32)[None, None, :]).astype(
        jnp.int32
    )
    flat_choice = choosers.reshape(2 * local_seqs, EXPERTS)
    earlier = jnp.cumsum(flat_choice, axis=0) - flat_choice
    slot_index = jnp.sum(earlier * flat_choice, axis=1)
    target = (routes.reshape(-1) * CAP + slot_index).reshape(local_seqs, 2)
    slot_ids = jnp.arange(EXPERTS * CAP, dtype=jnp.int32)
    placing = jnp.sum(
        (slot_ids[:, None, None] == target[None, :, :]).astype(jnp.float32), axis=2
    ).astype(jnp.bfloat16)
    mixing = jnp.sum(
        jnp.where(
            slot_ids[None, None, :] == target[:, :, None],
            route_weights.astype(jnp.float32)[:, :, None],
            jnp.float32(0.0),
        ),
        axis=1,
    ).astype(jnp.bfloat16)
    packed = jnp.dot(placing, scaled, preferred_element_type=jnp.float32).astype(jnp.bfloat16)
    flat = packed.reshape(EXPERTS, CAP * local_width // LANES, LANES)
    rows = between_segments(flat).reshape(EXPERTS * CAP, local_width)
    terms = through_expert(gathered(rows), gain, gate_weight, up_weight, down_weight)
    results = summed(terms).astype(jnp.bfloat16)
    results, mixing = lax.optimization_barrier((results, mixing))
    per_slot = between_segments(results.reshape(flat.shape)).reshape(EXPERTS * CAP, local_width)
    moe_sum = jnp.dot(mixing, per_slot, preferred_element_type=jnp.float32)
    return (residual + moe_sum).astype(jnp.bfloat16)


def solution(mesh):
    split = Mesh(
        mesh.devices.reshape(
            mesh.shape["parts"], EXPERTS, mesh.shape["expert"] // (2 * EXPERTS), 2, mesh.shape["tensor"]
        ),
        ("parts", "seg", "pos", "core", "tensor"),
    )
    return jax.shard_map(
        on_device,
        mesh=split,
        in_specs=(
            P(PARTS_EXPERT, "tensor"),
            P(PARTS_EXPERT, "tensor", None),
            P(None, PARTS_EXPERT, "tensor", None),
            P(None, PARTS_EXPERT, None, "tensor", None),
            P(PARTS_EXPERT),
            P("tensor"),
            P("tensor", EXPERT),
            P("tensor", EXPERT),
            P(EXPERT, "tensor"),
            P(PARTS_EXPERT, None),
            P(PARTS_EXPERT, None),
        ),
        out_specs=P(PARTS_EXPERT, "tensor"),
        check_vma=False,
    )
```

time: 266 us -> 225 us (0.85)
  blocking collectives: 34.8 us -> 119 us
  starting transfers between devices: 121 us -> 53.6 us
  waiting for transfers between devices: 86.1 us -> 38.5 us
  local copies, waits for them, and re-layouts: 11.7 us -> 2.81 us
    ppermute x6 -> x0, starting transfers between devices: 88.3 us -> none  [shifted(): return lax.ppermute(x, axis, [(i, (i + by) % count) for i in range(count)])]
    all_to_all x2 -> x4, blocking collectives: 34.8 us -> 119 us  [the longest x2 83.9 us: between_segments(): lax.all_to_all(blocks, EXPERT, split_axis=0, concat_axis=0, tiled=True, a...]
    ppermute x8 -> x14, waiting for transfers between devices: 64.5 us -> 38.5 us  [from_partner(): lax.ppermute(x, axis, [(i, i ^ apart) for i in range(lax.axis_size(axis))])]
    ppermute x6 -> x0, waiting for transfers between devices: 21.6 us -> none  [shifted(): return lax.ppermute(x, axis, [(i, (i + by) % count) for i in range(count)])]
    ppermute x8 -> x14, starting transfers between devices: 32.6 us -> 53.6 us  [from_partner(): lax.ppermute(x, axis, [(i, i ^ apart) for i in range(lax.axis_size(axis))])]
    concatenate x1, local copies, waits for them, and re-layouts: 7.68 us -> 0.02 us  [gathered(): following = jnp.concatenate([near_next, far_next], axis=0)]
  transfers between devices with their start and end apart: 14 -> 14, of which waited for: 11 -> 10; matrix products, arithmetic and copies ran while one was open for 0% -> 0% of each run, Pallas kernels for 0% -> 0%
where the time goes in v2:
time: 225 us; the launch traced here: 224 us
  blocking collectives  119 us (53%)
  starting transfers between devices  53.6 us (24%)
  waiting for transfers between devices  38.5 us (17%)
  matrix products  4.36 us (2%)
  local copies, waits for them, and re-layouts  2.81 us (1%)
  other arithmetic  2.78 us (1%)
  Pallas kernels  2.5 us (1%)
    all_to_all x2, blocking collectives, between_segments(): lax.all_to_all(blocks, EXPERT, split_axis=0, concat_axis=0, tiled=True, a...  83.9 us
    ppermute x14, starting transfers between devices, from_partner(): lax.ppermute(x, axis, [(i, i ^ apart) for i in range(lax.axis_size(axis))])  53.6 us
    ppermute x14, waiting for transfers between devices, from_partner(): lax.ppermute(x, axis, [(i, i ^ apart) for i in range(lax.axis_size(axis))])  38.5 us
    all_to_all x1, blocking collectives, through_expert(): lax.all_to_all(sums, 'tensor', split_axis=0, concat_axis=0, tiled=True)  22.8 us
    all_to_all x1, blocking collectives, through_expert(): lax.all_to_all(copies, 'tensor', split_axis=0, concat_axis=0, tiled=True)  12 us
  transfers between devices with their start and end apart: 14, of which 10 were waited for; matrix products, arithmetic and copies ran while one was open for 0% of the time, Pallas kernels for 0%

profile of v2, /device:TPU:40, one launch (start us, length us, event | category | flops | bytes accessed | tf_op | source)
XLA Modules:
  0.0 223.6 jit_solution(15521956241354591209)
XLA Ops:
  0.0 1.3 fusion.21
  1.3 0.7 iota_compare_fusion.3
  2.0 0.7 slice_bitcast_fusion
  2.7 1.0 fusion.8
  3.7 1.1 fusion.23
  4.8 0.2 fusion.7
  5.1 0.0 copy-start.5
  5.1 0.0 copy-start.3
  5.1 0.0 copy-start.4
  5.1 0.3 convolution_add_fusion.1
  5.4 0.4 copy-done.5
  5.7 0.1 copy.37
  5.8 0.1 eq.43
  5.9 0.1 fusion.14
  6.0 0.1 reduce_window_sum.11
  6.0 0.2 select_reduce_fusion.1
  6.2 0.1 reduce_sum.40
  6.3 0.1 copy.38
  6.4 0.1 convert_reduce_fusion
  6.5 0.0 copy-done.4
  6.5 0.2 convolution_convert_fusion
  6.7 0.2 reshape.70
  6.9 0.0 copy-start.1
  6.9 61.8 %all_to_all.20 = bf16[4,108,128]{2,1,0:T(8,128)(2,1)S(1)} all-to-all(bf16[4,108,128]{2,1,0:T(8,128)(2,1)S(1)} %reshape.70), channel_id=1, replica_groups={{0,64,160,224},{4,68,164,228},{8,72,168,232},{12,76,172,236},{16,80,176..., dimensions={0} | all-to-all | bytes 221184 | tf_op jit(solution)/shard_map/all_to_all | solution.py:69
  68.7 0.2 reshape.71
  68.8 13.5 %collective-permute-start = (bf16[36,1536]{1,0:T(8,128)(2,1)S(1)}, bf16[36,1536]{1,0:T(8,128)(2,1)S(1)}, u32[]{:S(2)}, u32[]{:S(2)}) collective-permute-start(bf16[36,1536]{1,0:T(8,128)(2,1)S(1)} %reshape.71), channel_id=1, source_target_pairs={{0,32},{8,40},{16,48},{24,56},{32,0},{40,8},{48,16},{56,24},{1,33}... | collective-permute-start | bytes 331784 | tf_op jit(solution)/shard_map/ppermute | solution.py:23
  82.4 2.3 %collective-permute-start.1 = (bf16[36,1536]{1,0:T(8,128)(2,1)S(1)}, bf16[36,1536]{1,0:T(8,128)(2,1)S(1)}, u32[]{:S(2)}, u32[]{:S(2)}) collective-permute-start(bf16[36,1536]{1,0:T(8,128)(2,1)S(1)} %reshape.71), channel_id=1, source_target_pairs={{0,16},{8,24},{16,0},{24,8},{32,48},{40,56},{48,32},{56,40},{1,17}... | collective-permute-start | bytes 331784 | tf_op jit(solution)/shard_map/ppermute | solution.py:23
  84.7 5.3 %collective-permute-done = bf16[36,1536]{1,0:T(8,128)(2,1)S(1)} collective-permute-done((bf16[36,1536]{1,0:T(8,128)(2,1)S(1)}, bf16[36,1536]{1,0:T(8,128)(2,1)S(1)}, u32[]{:S(2)}, u32[]{:S(2)}) %collective-permute-start) | collective-permute-done | bytes 110624 | tf_op jit(solution)/shard_map/ppermute | solution.py:23
  90.0 4.2 %collective-permute-start.2 = (bf16[36,1536]{1,0:T(8,128)(2,1)S(1)}, bf16[36,1536]{1,0:T(8,128)(2,1)S(1)}, u32[]{:S(2)}, u32[]{:S(2)}) collective-permute-start(bf16[36,1536]{1,0:T(8,128)(2,1)S(1)} %collective-permute-done), channel_id=1, source_target_pairs={{0,16},{8,24},{16,0},{24,8},{32,48},{40,56},{48,32},{56,40},{1,17}... | collective-permute-start | bytes 331784 | tf_op jit(solution)/shard_map/ppermute | solution.py:23
  94.2 2.7 %collective-permute-start.3 = (bf16[72,1536]{1,0:T(8,128)(2,1)S(1)}, bf16[72,1536]{1,0:T(8,128)(2,1)S(1)}, u32[]{:S(2)}, u32[]{:S(2)}) collective-permute-start(bf16[72,1536]{1,0:T(8,128)(2,1)S(1)} %pad_maximum_fusion.1), channel_id=1, source_target_pairs={{0,8},{8,0},{16,24},{24,16},{32,40},{40,32},{48,56},{56,48},{1,9},... | collective-permute-start | bytes 663560 | tf_op jit(solution)/shard_map/ppermute | solution.py:23
  97.0 2.3 %collective-permute-done.2 = bf16[36,1536]{1,0:T(8,128)(2,1)S(1)} collective-permute-done((bf16[36,1536]{1,0:T(8,128)(2,1)S(1)}, bf16[36,1536]{1,0:T(8,128)(2,1)S(1)}, u32[]{:S(2)}, u32[]{:S(2)}) %collective-permute-start.2) | collective-permute-done | bytes 110624 | tf_op jit(solution)/shard_map/ppermute | solution.py:23
  99.4 2.4 %collective-permute-start.4 = (bf16[72,1536]{1,0:T(8,128)(2,1)S(1)}, bf16[72,1536]{1,0:T(8,128)(2,1)S(1)}, u32[]{:S(2)}, u32[]{:S(2)}) collective-permute-start(bf16[72,1536]{1,0:T(8,128)(2,1)S(1)} %pad_maximum_fusion.2), channel_id=1, source_target_pairs={{0,8},{8,0},{16,24},{24,16},{32,40},{40,32},{48,56},{56,48},{1,9},... | collective-permute-start | bytes 663560 | tf_op jit(solution)/shard_map/ppermute | solution.py:23
  101.8 0.1 pad_maximum_fusion.refs_0_
  101.9 2.0 collective-permute-start.5
  103.8 0.6 collective-permute-done.3
  104.5 3.7 %collective-permute-done.4 = bf16[72,1536]{1,0:T(8,128)(2,1)S(1)} collective-permute-done((bf16[72,1536]{1,0:T(8,128)(2,1)S(1)}, bf16[72,1536]{1,0:T(8,128)(2,1)S(1)}, u32[]{:S(2)}, u32[]{:S(2)}) %collective-permute-start.4) | collective-permute-done | bytes 221216 | tf_op jit(solution)/shard_map/ppermute | solution.py:23
  108.2 2.0 collective-permute-start.6
  110.2 1.7 collective-permute-done.6.refs_3_
  112.0 2.2 up.1
  114.2 22.8 %all_to_all.21.sums_ref = bf16[4,144,1152]{2,1,0:T(8,128)(2,1)S(1)} all-to-all(bf16[4,144,1152]{2,1,0:T(8,128)(2,1)S(1)} %up.1), channel_id=1, replica_groups=mesh['parts'=2,'seg'=4,'pos'=8,'core'=2,'tensor'=4] {'tensor'}, dimensions={0} | all-to-all | bytes 2654208 | tf_op jit(solution)/shard_map/all_to_all | solution.py:183
  136.9 0.3 hidden.1
  137.2 12.0 %all_to_all.22 = bf16[4,144,512]{2,1,0:T(8,128)(2,1)S(1)} all-to-all(bf16[4,144,512]{2,1,0:T(8,128)(2,1)S(1)} %hidden.1), channel_id=1, replica_groups=mesh['parts'=2,'seg'=4,'pos'=8,'core'=2,'tensor'=4] {'tensor'}, dimensions={0} | all-to-all | bytes 1179648 | tf_op jit(solution)/shard_map/all_to_all | solution.py:185
  149.3 1.1 fusion.24
  150.4 0.1 fusion.19
  150.4 2.0 collective-permute-start.8
  152.4 2.4 %collective-permute-start.7 = (bf16[144,1536]{1,0:T(8,128)(2,1)S(1)}, bf16[144,1536]{1,0:T(8,128)(2,1)S(1)}, u32[]{:S(2)}, u32[]{:S(2)}) collective-permute-start(bf16[144,1536]{1,0:T(8,128)(2,1)S(1)} %get-tuple-element.12), channel_id=1, source_target_pairs={{0,4},{4,0},{1,5},{5,1},{2,6},{6,2},{3,7},{7,3},{8,12},{12,8},{9,1... | collective-permute-start | bytes 1327112 | tf_op jit(solution)/shard_map/ppermute | solution.py:23
  154.9 1.4 collective-permute-done.7
  156.2 0.2 fusion.2
  156.5 0.0 copy-start.6
  156.5 2.7 %collective-permute-start.10 = (bf16[72,1536]{1,0:T(8,128)(2,1)S(1)}, bf16[72,1536]{1,0:T(8,128)(2,1)S(1)}, u32[]{:S(2)}, u32[]{:S(2)}) collective-permute-start(bf16[72,1536]{1,0:T(8,128)(2,1)S(1)} %get-tuple-element.15), channel_id=1, source_target_pairs={{0,8},{8,0},{16,24},{24,16},{32,40},{40,32},{48,56},{56,48},{1,9},... | collective-permute-start | bytes 663560 | tf_op jit(solution)/shard_map/ppermute | solution.py:23
  159.2 3.2 %collective-permute-start.9 = (bf16[72,1536]{1,0:T(8,128)(2,1)S(1)}, bf16[72,1536]{1,0:T(8,128)(2,1)S(1)}, u32[]{:S(2)}, u32[]{:S(2)}) collective-permute-start(bf16[72,1536]{1,0:T(8,128)(2,1)S(1)} %get-tuple-element.16), channel_id=1, source_target_pairs={{0,8},{8,0},{16,24},{24,16},{32,40},{40,32},{48,56},{56,48},{1,9},... | collective-permute-start | bytes 663560 | tf_op jit(solution)/shard_map/ppermute | solution.py:23
  162.4 4.3 %collective-permute-done.10 = bf16[72,1536]{1,0:T(8,128)(2,1)S(1)} collective-permute-done((bf16[72,1536]{1,0:T(8,128)(2,1)S(1)}, bf16[72,1536]{1,0:T(8,128)(2,1)S(1)}, u32[]{:S(2)}, u32[]{:S(2)}) %collective-permute-start.10) | collective-permute-done | bytes 221216 | tf_op jit(solution)/shard_map/ppermute | solution.py:23
  166.7 4.1 %collective-permute-done.9 = bf16[72,1536]{1,0:T(8,128)(2,1)S(1)} collective-permute-done((bf16[72,1536]{1,0:T(8,128)(2,1)S(1)}, bf16[72,1536]{1,0:T(8,128)(2,1)S(1)}, u32[]{:S(2)}, u32[]{:S(2)}) %collective-permute-start.9) | collective-permute-done | bytes 221216 | tf_op jit(solution)/shard_map/ppermute | solution.py:23
  170.9 0.1 fusion.3
  171.0 4.3 %collective-permute-start.12 = (bf16[36,1536]{1,0:T(8,128)(2,1)S(1)}, bf16[36,1536]{1,0:T(8,128)(2,1)S(1)}, u32[]{:S(2)}, u32[]{:S(2)}) collective-permute-start(bf16[36,1536]{1,0:T(8,128)(2,1)S(1)} %get-tuple-element.20), channel_id=1, source_target_pairs={{0,16},{8,24},{16,0},{24,8},{32,48},{40,56},{48,32},{56,40},{1,17}... | collective-permute-start | bytes 331784 | tf_op jit(solution)/shard_map/ppermute | solution.py:23
  175.4 2.5 %collective-permute-start.11 = (bf16[36,1536]{1,0:T(8,128)(2,1)S(1)}, bf16[36,1536]{1,0:T(8,128)(2,1)S(1)}, u32[]{:S(2)}, u32[]{:S(2)}) collective-permute-start(bf16[36,1536]{1,0:T(8,128)(2,1)S(1)} %get-tuple-element.19), channel_id=1, source_target_pairs={{0,16},{8,24},{16,0},{24,8},{32,48},{40,56},{48,32},{56,40},{1,17}... | collective-permute-start | bytes 331784 | tf_op jit(solution)/shard_map/ppermute | solution.py:23
  177.9 7.0 %collective-permute-done.12 = bf16[36,1536]{1,0:T(8,128)(2,1)S(1)} collective-permute-done((bf16[36,1536]{1,0:T(8,128)(2,1)S(1)}, bf16[36,1536]{1,0:T(8,128)(2,1)S(1)}, u32[]{:S(2)}, u32[]{:S(2)}) %collective-permute-start.12) | collective-permute-done | bytes 110624 | tf_op jit(solution)/shard_map/ppermute | solution.py:23
  184.9 7.4 %collective-permute-start.13 = (bf16[36,1536]{1,0:T(8,128)(2,1)S(1)}, bf16[36,1536]{1,0:T(8,128)(2,1)S(1)}, u32[]{:S(2)}, u32[]{:S(2)}) collective-permute-start(bf16[36,1536]{1,0:T(8,128)(2,1)S(1)} %fusion.4), channel_id=1, source_target_pairs={{0,32},{8,40},{16,48},{24,56},{32,0},{40,8},{48,16},{56,24},{1,33}... | collective-permute-start | bytes 331784 | tf_op jit(solution)/shard_map/ppermute | solution.py:23
  192.3 0.1 select_reduce_fusion
  192.4 8.0 %collective-permute-done.13 = bf16[36,1536]{1,0:T(8,128)(2,1)S(1)} collective-permute-done((bf16[36,1536]{1,0:T(8,128)(2,1)S(1)}, bf16[36,1536]{1,0:T(8,128)(2,1)S(1)}, u32[]{:S(2)}, u32[]{:S(2)}) %collective-permute-start.13) | collective-permute-done | bytes 110624 | tf_op jit(solution)/shard_map/ppermute | solution.py:23
  200.4 0.2 reshape.73
  200.6 22.1 %all_to_all.23 = bf16[4,108,128]{2,1,0:T(8,128)(2,1)S(1)} all-to-all(bf16[4,108,128]{2,1,0:T(8,128)(2,1)S(1)} %reshape.73), channel_id=1, replica_groups={{0,64,160,224},{4,68,164,228},{8,72,168,232},{12,76,172,236},{16,80,176..., dimensions={0} | all-to-all | bytes 221184 | tf_op jit(solution)/shard_map/all_to_all | solution.py:69
  222.7 0.2 reshape.74
  222.9 0.8 fusion
  (25 shorter events, 0.4 us)
Async XLA Ops:
  0.0 149.3 %copy-start = (bf16[512,1536]{1,0:T(8,128)(2,1)S(1)}, bf16[512,1536]{1,0:T(8,128)(2,1)}, u32[]{:S(2)}) copy-start(bf16[512,1536]{1,0:T(8,128)(2,1)} %param.19) | copy-start | bytes 4718596
  5.1 0.7 copy-start.5
  5.1 1.4 copy-start.3
  5.1 1.4 copy-start.4
  6.9 105.1 %copy-start.1 = (bf16[1536,512]{1,0:T(8,128)(2,1)S(1)}, bf16[1536,512]{1,0:T(8,128)(2,1)}, u32[]{:S(2)}) copy-start(bf16[1536,512]{1,0:T(8,128)(2,1)} %refs_5_.1) | copy-start | bytes 4718596
  68.8 43.1 %copy-start.2 = (bf16[1536,512]{1,0:T(8,128)(2,1)S(1)}, bf16[1536,512]{1,0:T(8,128)(2,1)}, u32[]{:S(2)}) copy-start(bf16[1536,512]{1,0:T(8,128)(2,1)} %refs_6_.1) | copy-start | bytes 4718596
  68.8 21.1 %collective-permute-start = (bf16[36,1536]{1,0:T(8,128)(2,1)S(1)}, bf16[36,1536]{1,0:T(8,128)(2,1)S(1)}, u32[]{:S(2)}, u32[]{:S(2)}) collective-permute-start(bf16[36,1536]{1,0:T(8,128)(2,1)S(1)} %reshape.71), channel_id=1, source_target_pairs={{0,32},{8,40},{16,48},{24,56},{32,0},{40,8},{48,16},{56,24},{1,33}... | collective-permute-start | bytes 331784 | tf_op jit(solution)/shard_map/ppermute | solution.py:23
  82.4 14.6 %collective-permute-start.1 = (bf16[36,1536]{1,0:T(8,128)(2,1)S(1)}, bf16[36,1536]{1,0:T(8,128)(2,1)S(1)}, u32[]{:S(2)}, u32[]{:S(2)}) collective-permute-start(bf16[36,1536]{1,0:T(8,128)(2,1)S(1)} %reshape.71), channel_id=1, source_target_pairs={{0,16},{8,24},{16,0},{24,8},{32,48},{40,56},{48,32},{56,40},{1,17}... | collective-permute-start | bytes 331784 | tf_op jit(solution)/shard_map/ppermute | solution.py:23
  90.0 9.4 %collective-permute-start.2 = (bf16[36,1536]{1,0:T(8,128)(2,1)S(1)}, bf16[36,1536]{1,0:T(8,128)(2,1)S(1)}, u32[]{:S(2)}, u32[]{:S(2)}) collective-permute-start(bf16[36,1536]{1,0:T(8,128)(2,1)S(1)} %collective-permute-done), channel_id=1, source_target_pairs={{0,16},{8,24},{16,0},{24,8},{32,48},{40,56},{48,32},{56,40},{1,17}... | collective-permute-start | bytes 331784 | tf_op jit(solution)/shard_map/ppermute | solution.py:23
  94.2 10.2 %collective-permute-start.3 = (bf16[72,1536]{1,0:T(8,128)(2,1)S(1)}, bf16[72,1536]{1,0:T(8,128)(2,1)S(1)}, u32[]{:S(2)}, u32[]{:S(2)}) collective-permute-start(bf16[72,1536]{1,0:T(8,128)(2,1)S(1)} %pad_maximum_fusion.1), channel_id=1, source_target_pairs={{0,8},{8,0},{16,24},{24,16},{32,40},{40,32},{48,56},{56,48},{1,9},... | collective-permute-start | bytes 663560 | tf_op jit(solution)/shard_map/ppermute | solution.py:23
  99.4 8.8 %collective-permute-start.4 = (bf16[72,1536]{1,0:T(8,128)(2,1)S(1)}, bf16[72,1536]{1,0:T(8,128)(2,1)S(1)}, u32[]{:S(2)}, u32[]{:S(2)}) collective-permute-start(bf16[72,1536]{1,0:T(8,128)(2,1)S(1)} %pad_maximum_fusion.2), channel_id=1, source_target_pairs={{0,8},{8,0},{16,24},{24,16},{32,40},{40,32},{48,56},{56,48},{1,9},... | collective-permute-start | bytes 663560 | tf_op jit(solution)/shard_map/ppermute | solution.py:23
  101.9 8.3 %collective-permute-start.5 = (bf16[144,1536]{1,0:T(8,128)(2,1)S(1)}, bf16[144,1536]{1,0:T(8,128)(2,1)S(1)}, u32[]{:S(2)}, u32[]{:S(2)}) collective-permute-start(bf16[144,1536]{1,0:T(8,128)(2,1)S(1)} %pad_maximum_fusion.refs_0_), channel_id=1, source_target_pairs={{0,4},{4,0},{1,5},{5,1},{2,6},{6,2},{3,7},{7,3},{8,12},{12,8},{9,1... | collective-permute-start | bytes 1327112 | tf_op jit(solution)/shard_map/ppermute | solution.py:23
  108.2 3.7 %collective-permute-start.6 = (bf16[144,1536]{1,0:T(8,128)(2,1)S(1)}, bf16[144,1536]{1,0:T(8,128)(2,1)S(1)}, u32[]{:S(2)}, u32[]{:S(2)}) collective-permute-start(bf16[144,1536]{1,0:T(8,128)(2,1)S(1)} %constant_dynamic-update-slice_fusion.refs_1_), channel_id=1, source_target_pairs={{0,4},{4,0},{1,5},{5,1},{2,6},{6,2},{3,7},{7,3},{8,12},{12,8},{9,1... | collective-permute-start | bytes 1327112 | tf_op jit(solution)/shard_map/ppermute | solution.py:23
  150.4 4.4 %collective-permute-start.8 = (bf16[144,1536]{1,0:T(8,128)(2,1)S(1)}, bf16[144,1536]{1,0:T(8,128)(2,1)S(1)}, u32[]{:S(2)}, u32[]{:S(2)}) collective-permute-start(bf16[144,1536]{1,0:T(8,128)(2,1)S(1)} %get-tuple-element.11), channel_id=1, source_target_pairs={{0,4},{4,0},{1,5},{5,1},{2,6},{6,2},{3,7},{7,3},{8,12},{12,8},{9,1... | collective-permute-start | bytes 1327112 | tf_op jit(solution)/shard_map/ppermute | solution.py:23
  152.4 3.8 %collective-permute-start.7 = (bf16[144,1536]{1,0:T(8,128)(2,1)S(1)}, bf16[144,1536]{1,0:T(8,128)(2,1)S(1)}, u32[]{:S(2)}, u32[]{:S(2)}) collective-permute-start(bf16[144,1536]{1,0:T(8,128)(2,1)S(1)} %get-tuple-element.12), channel_id=1, source_target_pairs={{0,4},{4,0},{1,5},{5,1},{2,6},{6,2},{3,7},{7,3},{8,12},{12,8},{9,1... | collective-permute-start | bytes 1327112 | tf_op jit(solution)/shard_map/ppermute | solution.py:23
  156.5 18.9 %copy-start.6 = (bf16[16,2]{0,1:T(2,128)(2,1)S(1)}, bf16[16,2]{0,1:T(2,128)(2,1)}, u32[]{:S(2)}) copy-start(bf16[16,2]{0,1:T(2,128)(2,1)} %param.21) | copy-start | bytes 196
  156.5 10.2 %collective-permute-start.10 = (bf16[72,1536]{1,0:T(8,128)(2,1)S(1)}, bf16[72,1536]{1,0:T(8,128)(2,1)S(1)}, u32[]{:S(2)}, u32[]{:S(2)}) collective-permute-start(bf16[72,1536]{1,0:T(8,128)(2,1)S(1)} %get-tuple-element.15), channel_id=1, source_target_pairs={{0,8},{8,0},{16,24},{24,16},{32,40},{40,32},{48,56},{56,48},{1,9},... | collective-permute-start | bytes 663560 | tf_op jit(solution)/shard_map/ppermute | solution.py:23
  159.2 11.7 %collective-permute-start.9 = (bf16[72,1536]{1,0:T(8,128)(2,1)S(1)}, bf16[72,1536]{1,0:T(8,128)(2,1)S(1)}, u32[]{:S(2)}, u32[]{:S(2)}) collective-permute-start(bf16[72,1536]{1,0:T(8,128)(2,1)S(1)} %get-tuple-element.16), channel_id=1, source_target_pairs={{0,8},{8,0},{16,24},{24,16},{32,40},{40,32},{48,56},{56,48},{1,9},... | collective-permute-start | bytes 663560 | tf_op jit(solution)/shard_map/ppermute | solution.py:23
  171.0 13.8 %collective-permute-start.12 = (bf16[36,1536]{1,0:T(8,128)(2,1)S(1)}, bf16[36,1536]{1,0:T(8,128)(2,1)S(1)}, u32[]{:S(2)}, u32[]{:S(2)}) collective-permute-start(bf16[36,1536]{1,0:T(8,128)(2,1)S(1)} %get-tuple-element.20), channel_id=1, source_target_pairs={{0,16},{8,24},{16,0},{24,8},{32,48},{40,56},{48,32},{56,40},{1,17}... | collective-permute-start | bytes 331784 | tf_op jit(solution)/shard_map/ppermute | solution.py:23
  175.4 17.0 %collective-permute-start.11 = (bf16[36,1536]{1,0:T(8,128)(2,1)S(1)}, bf16[36,1536]{1,0:T(8,128)(2,1)S(1)}, u32[]{:S(2)}, u32[]{:S(2)}) collective-permute-start(bf16[36,1536]{1,0:T(8,128)(2,1)S(1)} %get-tuple-element.19), channel_id=1, source_target_pairs={{0,16},{8,24},{16,0},{24,8},{32,48},{40,56},{48,32},{56,40},{1,17}... | collective-permute-start | bytes 331784 | tf_op jit(solution)/shard_map/ppermute | solution.py:23
  184.9 15.4 %collective-permute-start.13 = (bf16[36,1536]{1,0:T(8,128)(2,1)S(1)}, bf16[36,1536]{1,0:T(8,128)(2,1)S(1)}, u32[]{:S(2)}, u32[]{:S(2)}) collective-permute-start(bf16[36,1536]{1,0:T(8,128)(2,1)S(1)} %fusion.4), channel_id=1, source_target_pairs={{0,32},{8,40},{16,48},{24,56},{32,0},{40,8},{48,16},{56,24},{1,33}... | collective-permute-start | bytes 331784 | tf_op jit(solution)/shard_map/ppermute | solution.py:23

commit v3 on v2

--- a/solution.py
+++ b/solution.py
@@ -161,19 +161,44 @@
     return held, following, held_there, following_there
 
 
-def summed(terms):
-    part = terms.shape[0] // 4
-    held, following, held_there, following_there = (
-        terms[i * part : (i + 1) * part] for i in range(4)
-    )
-    following = following + from_partner(send(following_there), "core", 1).astype(jnp.float32)
-    held = held + from_partner(send(held_there), "core", 1).astype(jnp.float32)
-    half = part // 2
-    far = held[half:] + from_partner(send(following[half:]), "pos", 1).astype(jnp.float32)
-    near = held[:half] + from_partner(send(following[:half]), "pos", 1).astype(jnp.float32)
+def down_kernel(hidden_ref, weight_ref, *outs):
+    count = hidden_ref.shape[1]
+    hidden = hidden_ref[...].reshape(-1, hidden_ref.shape[2])
+    width = weight_ref.shape[1] // 3
+    for start in range(0, 3 * width, width):
+        columns = slice(start, start + width)
+        terms = jnp.dot(hidden, weight_ref[:, columns], preferred_element_type=jnp.float32)
+        for i, out in enumerate(outs):
+            out[:, columns] = terms[i * count : (i + 1) * count].astype(out.dtype)
+
+
+def down_part(hidden, down_weight):
+    _, count, _ = hidden.shape
+    width = down_weight.shape[1]
+    whole = pl.BlockSpec(memory_space=pltpu.VMEM)
+    kinds = (jnp.float32, jnp.float32, jnp.bfloat16, jnp.bfloat16)
+    return pl.pallas_call(
+        down_kernel,
+        out_shape=[pltpu.VMEM((count, width), kind) for kind in kinds],
+        in_specs=[whole, whole],
+        out_specs=[whole] * len(kinds),
+        compiler_params=pltpu.CompilerParams(vmem_limit_bytes=16 << 20),
+        name="down",
+    )(kept(hidden), kept(down_weight))
+
+
+def summed(held, following, held_there, following_there):
+    half = held.shape[0] // 2
     own = half // 2
-    by4 = near[own:] + from_partner(send(far[own:]), "pos", 2).astype(jnp.float32)
-    home = near[:own] + from_partner(send(far[:own]), "pos", 2).astype(jnp.float32)
+    here = from_partner(following_there, "core", 1).astype(jnp.float32)
+    following = send(following + here)
+    held = held + from_partner(held_there, "core", 1).astype(jnp.float32)
+    near, far = lax.optimization_barrier((held[:half], held[half:]))
+    far = far + from_partner(following[half:], "pos", 1).astype(jnp.float32)
+    near = near + from_partner(following[:half], "pos", 1).astype(jnp.float32)
+    far = send(far)
+    by4 = near[own:] + from_partner(far[own:], "pos", 2).astype(jnp.float32)
+    home = near[:own] + from_partner(far[:own], "pos", 2).astype(jnp.float32)
     return home + from_partner(send(by4), "pos", 4).astype(jnp.float32)
 
 
@@ -183,8 +208,7 @@
     sums = lax.all_to_all(sums, "tensor", split_axis=0, concat_axis=0, tiled=True)
     copies = activated(sums, gate_weight.shape[0] * across)
     hidden = lax.all_to_all(copies, "tensor", split_axis=0, concat_axis=0, tiled=True)
-    hidden = hidden.reshape(-1, hidden.shape[2])
-    return jnp.dot(hidden, down_weight, preferred_element_type=jnp.float32)
+    return down_part(hidden, down_weight)
 
 
 def on_device(
@@ -226,7 +250,7 @@
     flat = packed.reshape(EXPERTS, CAP * local_width // LANES, LANES)
     rows = between_segments(flat).reshape(EXPERTS * CAP, local_width)
     terms = through_expert(gathered(rows), gain, gate_weight, up_weight, down_weight)
-    results = summed(terms).astype(jnp.bfloat16)
+    results = summed(*terms).astype(jnp.bfloat16)
     results, mixing = lax.optimization_barrier((results, mixing))
     per_slot = between_segments(results.reshape(flat.shape)).reshape(EXPERTS * CAP, local_width)
     moe_sum = jnp.dot(mixing, per_slot, preferred_element_type=jnp.float32)

time: 225 us -> 216 us (0.960)
  waiting for transfers between devices: 38.5 us -> 33 us
    ppermute x14, waiting for transfers between devices: 38.5 us -> 33 us  [from_partner(): lax.ppermute(x, axis, [(i, i ^ apart) for i in range(lax.axis_size(axis))])]
  transfers between devices with their start and end apart: 14 -> 14, of which waited for: 10 -> 8; matrix products, arithmetic and copies ran while one was open for 0% -> 0% of each run, Pallas kernels for 0% -> 0%
where the time goes in v3:
time: 216 us; the launch traced here: 215 us
  blocking collectives  117 us (54%)
  starting transfers between devices  52 us (24%)
  waiting for transfers between devices  33 us (15%)
  Pallas kernels  3.58 us (2%)
  matrix products  3.27 us (2%)
  other arithmetic  2.72 us (1%)
  local copies, waits for them, and re-layouts  2.69 us (1%)
    all_to_all x2, blocking collectives, between_segments(): lax.all_to_all(blocks, EXPERT, split_axis=0, concat_axis=0, tiled=True, a...  82.5 us
    ppermute x14, starting transfers between devices, from_partner(): lax.ppermute(x, axis, [(i, i ^ apart) for i in range(lax.axis_size(axis))])  52 us
    ppermute x14, waiting for transfers between devices, from_partner(): lax.ppermute(x, axis, [(i, i ^ apart) for i in range(lax.axis_size(axis))])  33 us
    all_to_all x1, blocking collectives, through_expert(): lax.all_to_all(sums, 'tensor', split_axis=0, concat_axis=0, tiled=True)  22.8 us
    all_to_all x1, blocking collectives, through_expert(): lax.all_to_all(copies, 'tensor', split_axis=0, concat_axis=0, tiled=True)  12.2 us
  transfers between devices with their start and end apart: 14, of which 8 were waited for; matrix products, arithmetic and copies ran while one was open for 0% of the time, Pallas kernels for 0%

profile of v3, /device:TPU:40, one launch (start us, length us, event | category | flops | bytes accessed | tf_op | source)
XLA Modules:
  0.0 215.2 jit_solution(16529911770130088828)
XLA Ops:
  0.0 1.1 fusion.19
  1.2 0.7 iota_compare_fusion.3
  1.9 0.7 slice_bitcast_fusion
  2.6 1.0 fusion.6
  3.6 1.1 fusion.21
  4.7 0.2 fusion.5
  4.9 0.0 copy-start.5
  5.0 0.0 copy-start.3
  5.0 0.0 copy-start.4
  5.0 0.3 convolution_add_fusion.1
  5.3 0.4 copy-done.5
  5.6 0.1 copy.37
  5.7 0.1 eq.43
  5.8 0.1 fusion.12
  5.9 0.1 reduce_window_sum.11
  5.9 0.2 select_reduce_fusion.1
  6.1 0.1 reduce_sum.40
  6.2 0.1 copy.38
  6.3 0.1 convert_reduce_fusion
  6.4 0.0 copy-done.4
  6.4 0.2 convolution_convert_fusion
  6.6 0.2 reshape.67
  6.8 0.0 copy-start.1
  6.8 0.0 copy-start.2
  6.8 61.9 %all_to_all.20 = bf16[4,108,128]{2,1,0:T(8,128)(2,1)S(1)} all-to-all(bf16[4,108,128]{2,1,0:T(8,128)(2,1)S(1)} %reshape.67), channel_id=1, replica_groups={{0,64,160,224},{4,68,164,228},{8,72,168,232},{12,76,172,236},{16,80,176..., dimensions={0} | all-to-all | bytes 221184 | tf_op jit(solution)/shard_map/all_to_all | solution.py:69
  68.7 0.2 reshape.68
  68.8 13.4 %collective-permute-start = (bf16[36,1536]{1,0:T(8,128)(2,1)S(1)}, bf16[36,1536]{1,0:T(8,128)(2,1)S(1)}, u32[]{:S(2)}, u32[]{:S(2)}) collective-permute-start(bf16[36,1536]{1,0:T(8,128)(2,1)S(1)} %reshape.68), channel_id=1, source_target_pairs={{0,32},{8,40},{16,48},{24,56},{32,0},{40,8},{48,16},{56,24},{1,33}... | collective-permute-start | bytes 331784 | tf_op jit(solution)/shard_map/ppermute | solution.py:23
  82.2 2.3 %collective-permute-start.1 = (bf16[36,1536]{1,0:T(8,128)(2,1)S(1)}, bf16[36,1536]{1,0:T(8,128)(2,1)S(1)}, u32[]{:S(2)}, u32[]{:S(2)}) collective-permute-start(bf16[36,1536]{1,0:T(8,128)(2,1)S(1)} %reshape.68), channel_id=1, source_target_pairs={{0,16},{8,24},{16,0},{24,8},{32,48},{40,56},{48,32},{56,40},{1,17}... | collective-permute-start | bytes 331784 | tf_op jit(solution)/shard_map/ppermute | solution.py:23
  84.6 5.3 %collective-permute-done = bf16[36,1536]{1,0:T(8,128)(2,1)S(1)} collective-permute-done((bf16[36,1536]{1,0:T(8,128)(2,1)S(1)}, bf16[36,1536]{1,0:T(8,128)(2,1)S(1)}, u32[]{:S(2)}, u32[]{:S(2)}) %collective-permute-start) | collective-permute-done | bytes 110624 | tf_op jit(solution)/shard_map/ppermute | solution.py:23
  89.9 4.2 %collective-permute-start.2 = (bf16[36,1536]{1,0:T(8,128)(2,1)S(1)}, bf16[36,1536]{1,0:T(8,128)(2,1)S(1)}, u32[]{:S(2)}, u32[]{:S(2)}) collective-permute-start(bf16[36,1536]{1,0:T(8,128)(2,1)S(1)} %collective-permute-done), channel_id=1, source_target_pairs={{0,16},{8,24},{16,0},{24,8},{32,48},{40,56},{48,32},{56,40},{1,17}... | collective-permute-start | bytes 331784 | tf_op jit(solution)/shard_map/ppermute | solution.py:23
  94.1 2.7 %collective-permute-start.3 = (bf16[72,1536]{1,0:T(8,128)(2,1)S(1)}, bf16[72,1536]{1,0:T(8,128)(2,1)S(1)}, u32[]{:S(2)}, u32[]{:S(2)}) collective-permute-start(bf16[72,1536]{1,0:T(8,128)(2,1)S(1)} %pad_maximum_fusion.1), channel_id=1, source_target_pairs={{0,8},{8,0},{16,24},{24,16},{32,40},{40,32},{48,56},{56,48},{1,9},... | collective-permute-start | bytes 663560 | tf_op jit(solution)/shard_map/ppermute | solution.py:23
  96.9 2.3 %collective-permute-done.2 = bf16[36,1536]{1,0:T(8,128)(2,1)S(1)} collective-permute-done((bf16[36,1536]{1,0:T(8,128)(2,1)S(1)}, bf16[36,1536]{1,0:T(8,128)(2,1)S(1)}, u32[]{:S(2)}, u32[]{:S(2)}) %collective-permute-start.2) | collective-permute-done | bytes 110624 | tf_op jit(solution)/shard_map/ppermute | solution.py:23
  99.3 2.4 %collective-permute-start.4 = (bf16[72,1536]{1,0:T(8,128)(2,1)S(1)}, bf16[72,1536]{1,0:T(8,128)(2,1)S(1)}, u32[]{:S(2)}, u32[]{:S(2)}) collective-permute-start(bf16[72,1536]{1,0:T(8,128)(2,1)S(1)} %pad_maximum_fusion.2), channel_id=1, source_target_pairs={{0,8},{8,0},{16,24},{24,16},{32,40},{40,32},{48,56},{56,48},{1,9},... | collective-permute-start | bytes 663560 | tf_op jit(solution)/shard_map/ppermute | solution.py:23
  101.7 0.1 pad_maximum_fusion.refs_0_
  101.8 2.0 collective-permute-start.5
  103.7 0.6 collective-permute-done.3
  104.4 3.7 %collective-permute-done.4 = bf16[72,1536]{1,0:T(8,128)(2,1)S(1)} collective-permute-done((bf16[72,1536]{1,0:T(8,128)(2,1)S(1)}, bf16[72,1536]{1,0:T(8,128)(2,1)S(1)}, u32[]{:S(2)}, u32[]{:S(2)}) %collective-permute-start.4) | collective-permute-done | bytes 221216 | tf_op jit(solution)/shard_map/ppermute | solution.py:23
  108.1 2.0 collective-permute-start.6
  110.1 1.7 collective-permute-done.6.refs_3_
  111.8 2.2 %up.1 = bf16[4,144,1152]{2,1,0:T(8,128)(2,1)S(1)} custom-call(bf16[144,1536]{1,0:T(8,128)(2,1)S(1)} %pad_maximum_fusion.refs_0_, bf16[144,1536]{1,0:T(8,128)(2,1)S(1)} %constant_dynamic-update-slice_fusion.refs_1_, bf16[144,1536]{1,0:T(8,128)(2,1)S(1)} %collective-permute-done.5.refs_2_, bf16[144,1536]{1,0:T(8,128)(2,1)S(1)} %collective-permute-done.6.refs_3_, ...), custom_call_target="tpu_custom_call" | custom-call | tf_op jit(solution)/shard_map/up/pallas_call | solution.py:106
  114.0 22.8 %all_to_all.21.sums_ref = bf16[4,144,1152]{2,1,0:T(8,128)(2,1)S(1)} all-to-all(bf16[4,144,1152]{2,1,0:T(8,128)(2,1)S(1)} %up.1), channel_id=1, replica_groups=mesh['parts'=2,'seg'=4,'pos'=8,'core'=2,'tensor'=4] {'tensor'}, dimensions={0} | all-to-all | bytes 2654208 | tf_op jit(solution)/shard_map/all_to_all | solution.py:208
  136.8 0.3 hidden.1
  137.1 0.0 copy-start.6
  137.1 12.2 %all_to_all.22.hidden_ref = bf16[4,144,512]{2,1,0:T(8,128)(2,1)S(1)} all-to-all(bf16[4,144,512]{2,1,0:T(8,128)(2,1)S(1)} %hidden.1), channel_id=1, replica_groups=mesh['parts'=2,'seg'=4,'pos'=8,'core'=2,'tensor'=4] {'tensor'}, dimensions={0} | all-to-all | bytes 1179648 | tf_op jit(solution)/shard_map/all_to_all | solution.py:210
  149.3 1.1 down.1
  150.4 2.0 collective-permute-start.8
  152.4 2.4 %collective-permute-start.7 = (bf16[144,1536]{1,0:T(8,128)(2,1)S(1)}, bf16[144,1536]{1,0:T(8,128)(2,1)S(1)}, u32[]{:S(2)}, u32[]{:S(2)}) collective-permute-start(bf16[144,1536]{1,0:T(8,128)(2,1)S(1)} %get-tuple-element.14), channel_id=1, source_target_pairs={{0,4},{4,0},{1,5},{5,1},{2,6},{6,2},{3,7},{7,3},{8,12},{12,8},{9,1... | collective-permute-start | bytes 1327112 | tf_op jit(solution)/shard_map/ppermute | solution.py:23
  154.8 0.1 add_convert_fusion
  154.9 2.7 %collective-permute-start.10 = (bf16[72,1536]{1,0:T(8,128)(2,1)S(1)}, bf16[72,1536]{1,0:T(8,128)(2,1)S(1)}, u32[]{:S(2)}, u32[]{:S(2)}) collective-permute-start(bf16[72,1536]{1,0:T(8,128)(2,1)S(1)} %get-tuple-element.23), channel_id=1, source_target_pairs={{0,8},{8,0},{16,24},{24,16},{32,40},{40,32},{48,56},{56,48},{1,9},... | collective-permute-start | bytes 663560 | tf_op jit(solution)/shard_map/ppermute | solution.py:23
  157.6 0.1 convert_add_fusion
  157.7 0.1 fusion.17
  157.8 3.2 %collective-permute-start.9 = (bf16[72,1536]{1,0:T(8,128)(2,1)S(1)}, bf16[72,1536]{1,0:T(8,128)(2,1)S(1)}, u32[]{:S(2)}, u32[]{:S(2)}) collective-permute-start(bf16[72,1536]{1,0:T(8,128)(2,1)S(1)} %get-tuple-element.24), channel_id=1, source_target_pairs={{0,8},{8,0},{16,24},{24,16},{32,40},{40,32},{48,56},{56,48},{1,9},... | collective-permute-start | bytes 663560 | tf_op jit(solution)/shard_map/ppermute | solution.py:23
  161.0 4.1 %collective-permute-done.10 = bf16[72,1536]{1,0:T(8,128)(2,1)S(1)} collective-permute-done((bf16[72,1536]{1,0:T(8,128)(2,1)S(1)}, bf16[72,1536]{1,0:T(8,128)(2,1)S(1)}, u32[]{:S(2)}, u32[]{:S(2)}) %collective-permute-start.10) | collective-permute-done | bytes 221216 | tf_op jit(solution)/shard_map/ppermute | solution.py:23
  165.2 4.3 %collective-permute-start.12 = (bf16[36,1536]{1,0:T(8,128)(2,1)S(1)}, bf16[36,1536]{1,0:T(8,128)(2,1)S(1)}, u32[]{:S(2)}, u32[]{:S(2)}) collective-permute-start(bf16[36,1536]{1,0:T(8,128)(2,1)S(1)} %get-tuple-element.28), channel_id=1, source_target_pairs={{0,16},{8,24},{16,0},{24,8},{32,48},{40,56},{48,32},{56,40},{1,17}... | collective-permute-start | bytes 331784 | tf_op jit(solution)/shard_map/ppermute | solution.py:23
  169.6 2.5 %collective-permute-start.11 = (bf16[36,1536]{1,0:T(8,128)(2,1)S(1)}, bf16[36,1536]{1,0:T(8,128)(2,1)S(1)}, u32[]{:S(2)}, u32[]{:S(2)}) collective-permute-start(bf16[36,1536]{1,0:T(8,128)(2,1)S(1)} %get-tuple-element.27), channel_id=1, source_target_pairs={{0,16},{8,24},{16,0},{24,8},{32,48},{40,56},{48,32},{56,40},{1,17}... | collective-permute-start | bytes 331784 | tf_op jit(solution)/shard_map/ppermute | solution.py:23
  172.1 0.1 convert_add_fusion.1
  172.1 4.9 %collective-permute-done.12 = bf16[36,1536]{1,0:T(8,128)(2,1)S(1)} collective-permute-done((bf16[36,1536]{1,0:T(8,128)(2,1)S(1)}, bf16[36,1536]{1,0:T(8,128)(2,1)S(1)}, u32[]{:S(2)}, u32[]{:S(2)}) %collective-permute-start.12) | collective-permute-done | bytes 110624 | tf_op jit(solution)/shard_map/ppermute | solution.py:23
  177.1 6.0 %collective-permute-start.13 = (bf16[36,1536]{1,0:T(8,128)(2,1)S(1)}, bf16[36,1536]{1,0:T(8,128)(2,1)S(1)}, u32[]{:S(2)}, u32[]{:S(2)}) collective-permute-start(bf16[36,1536]{1,0:T(8,128)(2,1)S(1)} %fusion.2), channel_id=1, source_target_pairs={{0,32},{8,40},{16,48},{24,56},{32,0},{40,8},{48,16},{56,24},{1,33}... | collective-permute-start | bytes 331784 | tf_op jit(solution)/shard_map/ppermute | solution.py:23
  183.1 0.1 select_reduce_fusion
  183.2 10.2 %collective-permute-done.13 = bf16[36,1536]{1,0:T(8,128)(2,1)S(1)} collective-permute-done((bf16[36,1536]{1,0:T(8,128)(2,1)S(1)}, bf16[36,1536]{1,0:T(8,128)(2,1)S(1)}, u32[]{:S(2)}, u32[]{:S(2)}) %collective-permute-start.13) | collective-permute-done | bytes 110624 | tf_op jit(solution)/shard_map/ppermute | solution.py:23
  193.4 0.2 reshape.69
  193.6 20.6 %all_to_all.23 = bf16[4,108,128]{2,1,0:T(8,128)(2,1)S(1)} all-to-all(bf16[4,108,128]{2,1,0:T(8,128)(2,1)S(1)} %reshape.69), channel_id=1, replica_groups={{0,64,160,224},{4,68,164,228},{8,72,168,232},{12,76,172,236},{16,80,176..., dimensions={0} | all-to-all | bytes 221184 | tf_op jit(solution)/shard_map/all_to_all | solution.py:69
  214.2 0.2 reshape.70
  214.4 0.8 fusion
  (27 shorter events, 0.4 us)
Async XLA Ops:
  4.9 0.7 copy-start.5
  5.0 1.4 copy-start.3
  5.0 1.4 copy-start.4
  6.8 105.1 %copy-start.1 = (bf16[1536,512]{1,0:T(8,128)(2,1)S(1)}, bf16[1536,512]{1,0:T(8,128)(2,1)}, u32[]{:S(2)}) copy-start(bf16[1536,512]{1,0:T(8,128)(2,1)} %refs_5_.1) | copy-start | bytes 4718596
  6.8 105.1 %copy-start.2 = (bf16[1536,512]{1,0:T(8,128)(2,1)S(1)}, bf16[1536,512]{1,0:T(8,128)(2,1)}, u32[]{:S(2)}) copy-start(bf16[1536,512]{1,0:T(8,128)(2,1)} %refs_6_.1) | copy-start | bytes 4718596
  68.8 21.0 %collective-permute-start = (bf16[36,1536]{1,0:T(8,128)(2,1)S(1)}, bf16[36,1536]{1,0:T(8,128)(2,1)S(1)}, u32[]{:S(2)}, u32[]{:S(2)}) collective-permute-start(bf16[36,1536]{1,0:T(8,128)(2,1)S(1)} %reshape.68), channel_id=1, source_target_pairs={{0,32},{8,40},{16,48},{24,56},{32,0},{40,8},{48,16},{56,24},{1,33}... | collective-permute-start | bytes 331784 | tf_op jit(solution)/shard_map/ppermute | solution.py:23
  82.2 14.6 %collective-permute-start.1 = (bf16[36,1536]{1,0:T(8,128)(2,1)S(1)}, bf16[36,1536]{1,0:T(8,128)(2,1)S(1)}, u32[]{:S(2)}, u32[]{:S(2)}) collective-permute-start(bf16[36,1536]{1,0:T(8,128)(2,1)S(1)} %reshape.68), channel_id=1, source_target_pairs={{0,16},{8,24},{16,0},{24,8},{32,48},{40,56},{48,32},{56,40},{1,17}... | collective-permute-start | bytes 331784 | tf_op jit(solution)/shard_map/ppermute | solution.py:23
  89.9 9.4 %collective-permute-start.2 = (bf16[36,1536]{1,0:T(8,128)(2,1)S(1)}, bf16[36,1536]{1,0:T(8,128)(2,1)S(1)}, u32[]{:S(2)}, u32[]{:S(2)}) collective-permute-start(bf16[36,1536]{1,0:T(8,128)(2,1)S(1)} %collective-permute-done), channel_id=1, source_target_pairs={{0,16},{8,24},{16,0},{24,8},{32,48},{40,56},{48,32},{56,40},{1,17}... | collective-permute-start | bytes 331784 | tf_op jit(solution)/shard_map/ppermute | solution.py:23
  94.1 10.2 %collective-permute-start.3 = (bf16[72,1536]{1,0:T(8,128)(2,1)S(1)}, bf16[72,1536]{1,0:T(8,128)(2,1)S(1)}, u32[]{:S(2)}, u32[]{:S(2)}) collective-permute-start(bf16[72,1536]{1,0:T(8,128)(2,1)S(1)} %pad_maximum_fusion.1), channel_id=1, source_target_pairs={{0,8},{8,0},{16,24},{24,16},{32,40},{40,32},{48,56},{56,48},{1,9},... | collective-permute-start | bytes 663560 | tf_op jit(solution)/shard_map/ppermute | solution.py:23
  99.3 8.8 %collective-permute-start.4 = (bf16[72,1536]{1,0:T(8,128)(2,1)S(1)}, bf16[72,1536]{1,0:T(8,128)(2,1)S(1)}, u32[]{:S(2)}, u32[]{:S(2)}) collective-permute-start(bf16[72,1536]{1,0:T(8,128)(2,1)S(1)} %pad_maximum_fusion.2), channel_id=1, source_target_pairs={{0,8},{8,0},{16,24},{24,16},{32,40},{40,32},{48,56},{56,48},{1,9},... | collective-permute-start | bytes 663560 | tf_op jit(solution)/shard_map/ppermute | solution.py:23
  101.8 8.3 %collective-permute-start.5 = (bf16[144,1536]{1,0:T(8,128)(2,1)S(1)}, bf16[144,1536]{1,0:T(8,128)(2,1)S(1)}, u32[]{:S(2)}, u32[]{:S(2)}) collective-permute-start(bf16[144,1536]{1,0:T(8,128)(2,1)S(1)} %pad_maximum_fusion.refs_0_), channel_id=1, source_target_pairs={{0,4},{4,0},{1,5},{5,1},{2,6},{6,2},{3,7},{7,3},{8,12},{12,8},{9,1... | collective-permute-start | bytes 1327112 | tf_op jit(solution)/shard_map/ppermute | solution.py:23
  108.1 3.7 %collective-permute-start.6 = (bf16[144,1536]{1,0:T(8,128)(2,1)S(1)}, bf16[144,1536]{1,0:T(8,128)(2,1)S(1)}, u32[]{:S(2)}, u32[]{:S(2)}) collective-permute-start(bf16[144,1536]{1,0:T(8,128)(2,1)S(1)} %constant_dynamic-update-slice_fusion.refs_1_), channel_id=1, source_target_pairs={{0,4},{4,0},{1,5},{5,1},{2,6},{6,2},{3,7},{7,3},{8,12},{12,8},{9,1... | collective-permute-start | bytes 1327112 | tf_op jit(solution)/shard_map/ppermute | solution.py:23
  136.8 12.5 %copy-start = (bf16[512,1536]{1,0:T(8,128)(2,1)S(1)}, bf16[512,1536]{1,0:T(8,128)(2,1)}, u32[]{:S(2)}) copy-start(bf16[512,1536]{1,0:T(8,128)(2,1)} %weight_ref.1) | copy-start | bytes 4718596
  137.1 15.2 %copy-start.6 = (bf16[16,2]{0,1:T(2,128)(2,1)S(1)}, bf16[16,2]{0,1:T(2,128)(2,1)}, u32[]{:S(2)}) copy-start(bf16[16,2]{0,1:T(2,128)(2,1)} %param.21) | copy-start | bytes 196
  150.4 4.4 %collective-permute-start.8 = (bf16[144,1536]{1,0:T(8,128)(2,1)S(1)}, bf16[144,1536]{1,0:T(8,128)(2,1)S(1)}, u32[]{:S(2)}, u32[]{:S(2)}) collective-permute-start(bf16[144,1536]{1,0:T(8,128)(2,1)S(1)} %get-tuple-element.17), channel_id=1, source_target_pairs={{0,4},{4,0},{1,5},{5,1},{2,6},{6,2},{3,7},{7,3},{8,12},{12,8},{9,1... | collective-permute-start | bytes 1327112 | tf_op jit(solution)/shard_map/ppermute | solution.py:23
  152.4 5.3 %collective-permute-start.7 = (bf16[144,1536]{1,0:T(8,128)(2,1)S(1)}, bf16[144,1536]{1,0:T(8,128)(2,1)S(1)}, u32[]{:S(2)}, u32[]{:S(2)}) collective-permute-start(bf16[144,1536]{1,0:T(8,128)(2,1)S(1)} %get-tuple-element.14), channel_id=1, source_target_pairs={{0,4},{4,0},{1,5},{5,1},{2,6},{6,2},{3,7},{7,3},{8,12},{12,8},{9,1... | collective-permute-start | bytes 1327112 | tf_op jit(solution)/shard_map/ppermute | solution.py:23
  154.9 10.2 %collective-permute-start.10 = (bf16[72,1536]{1,0:T(8,128)(2,1)S(1)}, bf16[72,1536]{1,0:T(8,128)(2,1)S(1)}, u32[]{:S(2)}, u32[]{:S(2)}) collective-permute-start(bf16[72,1536]{1,0:T(8,128)(2,1)S(1)} %get-tuple-element.23), channel_id=1, source_target_pairs={{0,8},{8,0},{16,24},{24,16},{32,40},{40,32},{48,56},{56,48},{1,9},... | collective-permute-start | bytes 663560 | tf_op jit(solution)/shard_map/ppermute | solution.py:23
  157.8 14.3 %collective-permute-start.9 = (bf16[72,1536]{1,0:T(8,128)(2,1)S(1)}, bf16[72,1536]{1,0:T(8,128)(2,1)S(1)}, u32[]{:S(2)}, u32[]{:S(2)}) collective-permute-start(bf16[72,1536]{1,0:T(8,128)(2,1)S(1)} %get-tuple-element.24), channel_id=1, source_target_pairs={{0,8},{8,0},{16,24},{24,16},{32,40},{40,32},{48,56},{56,48},{1,9},... | collective-permute-start | bytes 663560 | tf_op jit(solution)/shard_map/ppermute | solution.py:23
  165.2 11.8 %collective-permute-start.12 = (bf16[36,1536]{1,0:T(8,128)(2,1)S(1)}, bf16[36,1536]{1,0:T(8,128)(2,1)S(1)}, u32[]{:S(2)}, u32[]{:S(2)}) collective-permute-start(bf16[36,1536]{1,0:T(8,128)(2,1)S(1)} %get-tuple-element.28), channel_id=1, source_target_pairs={{0,16},{8,24},{16,0},{24,8},{32,48},{40,56},{48,32},{56,40},{1,17}... | collective-permute-start | bytes 331784 | tf_op jit(solution)/shard_map/ppermute | solution.py:23
  169.6 13.6 %collective-permute-start.11 = (bf16[36,1536]{1,0:T(8,128)(2,1)S(1)}, bf16[36,1536]{1,0:T(8,128)(2,1)S(1)}, u32[]{:S(2)}, u32[]{:S(2)}) collective-permute-start(bf16[36,1536]{1,0:T(8,128)(2,1)S(1)} %get-tuple-element.27), channel_id=1, source_target_pairs={{0,16},{8,24},{16,0},{24,8},{32,48},{40,56},{48,32},{56,40},{1,17}... | collective-permute-start | bytes 331784 | tf_op jit(solution)/shard_map/ppermute | solution.py:23
  177.1 16.3 %collective-permute-start.13 = (bf16[36,1536]{1,0:T(8,128)(2,1)S(1)}, bf16[36,1536]{1,0:T(8,128)(2,1)S(1)}, u32[]{:S(2)}, u32[]{:S(2)}) collective-permute-start(bf16[36,1536]{1,0:T(8,128)(2,1)S(1)} %fusion.2), channel_id=1, source_target_pairs={{0,32},{8,40},{16,48},{24,56},{32,0},{40,8},{48,16},{56,24},{1,33}... | collective-permute-start | bytes 331784 | tf_op jit(solution)/shard_map/ppermute | solution.py:23
